TPU v7x, 32 devices: a whole 2x2x4 slice. The times are simulated.
32 devices in a mesh: ctx: 8 (over y, x, core), head: 4 (over z).
Axes of the slice: x: 2, y: 2, z: 4, core: 2. Of those that a mesh axis runs over, the one named last changes fastest.
Arguments:
- tokens: bfloat16 [2048, 3072], P('ctx', 'head'), may hold values from -6 to 6
- w_qkv: bfloat16 [3, 3072, 3072], P(None, None, 'head'), may hold values from -0.109375 to 0.109375
- w_out: bfloat16 [3072, 3072], P('head'), may hold values from -2 to 2
- block_perm: int32 [32], replicated, may hold values from 0 to 31, as said below
Outputs:
- mixed: bfloat16 [2048, 3072], P('ctx', 'head')
Inputs may be any that keep to these rules, and one draw needn't show every extreme that they name: A permutation; slot s holds frame row block_perm[s], token rows s * 64 to (s + 1) * 64 - 1 of tokens. Cut the frame rows into 16 runs of 2 consecutive rows, numbered 0 up; each index of ctx holds, for one c of its own, run c in its first 2 slots and run 2 * 8 - 1 - c in its last 2 slots, in row order.
All inputs are finite; a program needn't handle non-finite values.
Results may differ from a plain program's by a relative error of at most 0.02.
Values may be sent and summed in bfloat16 or wider, within the bound.
No kernel may reach another device: no remote copies, remote signals or barrier semaphores. Data moves between devices by JAX's collectives and lax.ppermute only.
A program may use at most 192 MiB of HBM per device.

v0:
```python
import functools
import math

import jax
import jax.numpy as jnp
from jax import lax
from jax.experimental import pallas as pl
from jax.experimental.pallas import tpu as pltpu
from jax.sharding import PartitionSpec as P


HD = 128
WW = 64
F = 8
ROPE_BASE = 10000.0
EPSILON = 1e-06
CORES = 2
MASKED = -1e30
GRANT = 12 << 20


def part_sizes():
    return (HD // 16, 7 * HD // 32, 7 * HD // 32)


def rope_tables(slot_frame, slot_row):
    slots = slot_frame.shape[0]
    lane = lax.broadcasted_iota(jnp.int32, (slots, WW, HD), 2)
    column = lax.broadcasted_iota(jnp.int32, (slots, WW, HD), 1).astype(jnp.float32)
    frame = jnp.broadcast_to(slot_frame.astype(jnp.float32)[:, None, None], lane.shape)
    row = jnp.broadcast_to(slot_row.astype(jnp.float32)[:, None, None], lane.shape)
    p0, p1, p2 = part_sizes()
    first, second = 2 * p0, 2 * p0 + 2 * p1
    position = jnp.where(lane < first, frame, jnp.where(lane < second, row, column))
    freq, sign = [], []
    for pairs in (p0, p1, p2):
        steps = ROPE_BASE ** (-jnp.arange(pairs, dtype=jnp.float32) / pairs)
        freq += [steps, steps]
        sign += [-jnp.ones((pairs,), jnp.float32), jnp.ones((pairs,), jnp.float32)]
    angle = position * jnp.concatenate(freq)
    cosine = jnp.cos(angle).reshape(slots * WW, HD)
    sine = (jnp.sin(angle) * jnp.concatenate(sign)).reshape(slots * WW, HD)
    return cosine, sine


def norm_rotate(v, cosine, sine, scale):
    p0, p1, _ = part_sizes()
    mean = jnp.mean(v * v, axis=-1, keepdims=True)
    v = v * (lax.rsqrt(mean + EPSILON) * scale)
    lane = lax.broadcasted_iota(jnp.int32, v.shape, 1)
    low = (
        (lane < p0)
        | ((lane >= 2 * p0) & (lane < 2 * p0 + p1))
        | ((lane >= 2 * p0 + 2 * p1) & (lane < 2 * p0 + 3 * p1))
    )
    near = jnp.where(low, pltpu.roll(v, HD - p0, 1), pltpu.roll(v, p0, 1))
    far = jnp.where(low, pltpu.roll(v, HD - p1, 1), pltpu.roll(v, p1, 1))
    other = jnp.where(lane < 2 * p0, near, far)
    return v * cosine + other * sine


def vmem_call(body, inputs, outputs, smem=(), after=(), scratch=(), flops=0, grant=GRANT):
    vmem = pl.BlockSpec(memory_space=pltpu.VMEM)
    n_smem, n_after = len(smem), len(after)

    def kernel(*refs):
        body(*refs[:n_smem], *refs[n_smem + n_after :])

    single = len(outputs) == 1
    return pl.pallas_call(
        kernel,
        in_specs=[pl.BlockSpec(memory_space=pltpu.SMEM)] * n_smem
        + [pl.BlockSpec(memory_space=pl.ANY)] * n_after
        + [vmem] * len(inputs),
        out_specs=vmem if single else [vmem] * len(outputs),
        out_shape=outputs[0] if single else list(outputs),
        scratch_shapes=list(scratch),
        compiler_params=pltpu.CompilerParams(vmem_limit_bytes=grant),
        cost_estimate=pl.CostEstimate(flops=flops, bytes_accessed=0, transcendentals=0),
    )(*smem, *after, *inputs)


def fetch_kernel(cuts, *refs):
    count = len(cuts)
    sources, targets, sems = refs[:count], refs[count : 2 * count], refs[2 * count]
    core = lax.axis_index("ctx") % CORES
    copies = []
    for source, target, cut in zip(sources, targets, cuts):
        for at in range(target.shape[0]):
            view = source.at[at]
            if cut:
                width = target.shape[-1]
                cols = pl.ds(pl.multiple_of(core * width, width), width)
                view = source.at[at, :, cols]
            copies.append(pltpu.make_async_copy(view, target.at[at], sems.at[len(copies)]))
    for copy in copies:
        copy.start()
    for copy in copies:
        copy.wait()


def fetch(w_qkv, w_out, pieces):
    three, feats, cols = w_qkv.shape
    shapes = [(three, feats, cols // CORES), (pieces, w_out.shape[0] // pieces, w_out.shape[1])]
    any_space = pl.BlockSpec(memory_space=pltpu.MemorySpace.HBM)
    return pl.pallas_call(
        functools.partial(fetch_kernel, (True, False)),
        in_specs=[any_space] * 2,
        out_specs=[pl.BlockSpec(memory_space=pltpu.VMEM)] * 2,
        out_shape=[jax.ShapeDtypeStruct(shape, jnp.bfloat16) for shape in shapes],
        scratch_shapes=[pltpu.SemaphoreType.DMA((three + pieces,))],
        compiler_params=pltpu.CompilerParams(vmem_limit_bytes=46 << 20),
        name="fetch",
    )(w_qkv, w_out.reshape(shapes[1]))


def project_kernel(pieces, heads, shifts, kind, cos_ref, sin_ref, *refs):
    mine = refs[:pieces]
    theirs = refs[pieces : 2 * pieces]
    w_ref, out_ref = refs[2 * pieces :]
    _, feats = mine[0].shape
    width = heads * HD
    level = lax.axis_index("head")

    def product(j):
        total = None
        for i, k in enumerate(shifts):
            block = lax.rem(level - k + pieces, pieces)
            at = pl.ds(pl.multiple_of(block * feats, feats), feats)
            x = jnp.concatenate([mine[i][...], theirs[i][...]], axis=0)
            dot = jnp.dot(x, w_ref[j, at, :], preferred_element_type=jnp.float32)
            total = dot if total is None else total + dot
        return total

    scale = HD ** (-0.5) * math.log2(math.e) if kind == "q" else 1.0
    raw = product(0 if kind == "q" else 1)
    if kind == "kv":
        out_ref[:, pl.ds(width, width)] = product(2).astype(jnp.bfloat16)
    cosine, sine = cos_ref[...], sin_ref[...]
    for h in range(heads):
        v = norm_rotate(raw[:, h * HD : (h + 1) * HD], cosine, sine, scale)
        out_ref[:, pl.ds(h * HD, HD)] = v.astype(jnp.bfloat16)


def project(kind, shifts, mine, theirs, w_qkv, cosine, sine):
    pieces = len(mine)
    rows, feats = mine[0].shape
    width = w_qkv.shape[2]
    count = 1 if kind == "q" else 2
    return vmem_call(
        functools.partial(project_kernel, pieces, width // HD, shifts, kind),
        [cosine, sine, *mine, *theirs, w_qkv],
        [jax.ShapeDtypeStruct((2 * rows, count * width), jnp.bfloat16)],
        flops=2 * 2 * rows * feats * pieces * count * width,
    )


def attend_kernel(carried, final, free, masked, heads, part, local_slots, perm_ref, q_ref, *refs):
    state_ref = refs[0] if carried else None
    kv = refs[carried : carried + free + masked]
    out_ref = refs[-1]
    rows = q_ref.shape[0] // 2
    width = heads * HD
    frame_rows = perm_ref.shape[0] // F
    me = lax.axis_index("ctx")

    def frame(device):
        return perm_ref[device * local_slots + part * (local_slots // 2)] // frame_rows

    frames = [frame(me ^ m) for m in range(2 * masked)]
    for h in range(heads):
        cols = pl.ds(h * HD, HD)
        wide_cols = pl.ds(2 * h * HD, 2 * HD)
        for r in range(2):
            window = pl.ds(r * rows, rows)
            q = q_ref[window, cols]
            if carried:
                acc = state_ref[window, wide_cols]
            else:
                acc = jnp.zeros((rows, 2 * HD), jnp.float32)
            for i in range(free + masked):
                keys = kv[i][:, cols]
                values = kv[i][:, pl.ds(width + h * HD, HD)]
                scores = lax.dot_general(
                    q, keys, (((1,), (1,)), ((), ())), preferred_element_type=jnp.float32
                )
                if i >= free:
                    half = scores.shape[1] // 2
                    at = 2 * (i - free)
                    bias = [
                        jnp.where(frames[at + s] <= frames[r], jnp.float32(0), jnp.float32(MASKED))
                        for s in range(2)
                    ]
                    scores = jnp.concatenate(
                        [scores[:, :half] + bias[0], scores[:, half:] + bias[1]], axis=1
                    )
                weights = jnp.exp2(scores).astype(jnp.bfloat16)
                wide = jnp.concatenate([values, jnp.ones_like(values)], axis=1)
                acc += jnp.dot(weights, wide, preferred_element_type=jnp.float32)
            if final:
                out_ref[window, cols] = (acc[:, :HD] / acc[:, HD:]).astype(jnp.bfloat16)
            else:
                out_ref[window, wide_cols] = acc


def attend(block_perm, q, state, free, masked, part, local_slots, final):
    rows2, width = q.shape
    heads = width // HD
    keys = sum(p.shape[0] for p in free + masked)
    carried = 0 if state is None else 1
    if final:
        out = jax.ShapeDtypeStruct((rows2, width), jnp.bfloat16)
    else:
        out = jax.ShapeDtypeStruct((rows2, 2 * width), jnp.float32)
    return vmem_call(
        functools.partial(
            attend_kernel, carried, final, len(free), len(masked), heads, part, local_slots
        ),
        [q] + ([state] if carried else []) + free + masked,
        [out],
        smem=[block_perm],
        flops=8 * rows2 * keys * width,
    )


def output_kernel(shifts, mine_ref, theirs_ref, w_ref, *outs):
    levels = len(shifts)
    rows = theirs_ref.shape[0]
    width = mine_ref.shape[1]
    level = lax.axis_index("head")
    core = lax.axis_index("ctx") % CORES
    mine_at = pl.ds(pl.multiple_of(core * width, width), width)
    theirs_at = pl.ds(pl.multiple_of((1 - core) * width, width), width)
    mine = mine_ref[pl.ds(0, rows), :]
    theirs = theirs_ref[...]
    span = w_ref.shape[1] // levels
    for i, k in enumerate(shifts):
        block = lax.rem(level + k, levels)
        cols = pl.ds(pl.multiple_of(block * span, span), span)
        part = jnp.dot(mine, w_ref[mine_at, cols], preferred_element_type=jnp.float32)
        part += jnp.dot(theirs, w_ref[theirs_at, cols], preferred_element_type=jnp.float32)
        outs[i][...] = part.astype(outs[i].dtype)


def output_parts(shifts, mine, theirs, w_out):
    rows = theirs.shape[0]
    cols = w_out.shape[1] // len(shifts)
    return vmem_call(
        functools.partial(output_kernel, shifts),
        [mine, theirs, w_out],
        [
            jax.ShapeDtypeStruct((rows, cols), jnp.float32 if k == 0 else jnp.bfloat16)
            for k in shifts
        ],
        flops=2 * rows * w_out.shape[0] * w_out.shape[1],
    )


def finish_kernel(count, *refs):
    out_ref = refs[-1]
    rows = refs[0].shape[0]
    for part in range(2):
        group = refs[part * count : (part + 1) * count]
        total = group[0][...]
        for ref in group[1:]:
            total += ref[...].astype(jnp.float32)
        out_ref[pl.ds(part * rows, rows), :] = total.astype(out_ref.dtype)


def finish(first, second):
    rows, cols = first[0].shape
    return vmem_call(
        functools.partial(finish_kernel, len(first)),
        [*first, *second],
        [jax.ShapeDtypeStruct((2 * rows, cols), jnp.bfloat16)],
        flops=rows * cols,
    )


def per_device(ctx, levels, tokens, w_qkv, w_out, block_perm):
    rows = tokens.shape[0]
    half = rows // 2
    local_slots = rows // WW
    run_slots = local_slots // 2
    me = lax.axis_index("ctx")
    chips = ctx // CORES
    frame_rows = block_perm.shape[0] // F
    slot_frame = block_perm // frame_rows
    slot_row = block_perm % frame_rows

    shifts = sorted(range(1, levels), key=lambda k: (-min(k, levels - k), k))

    def over_levels(x, k):
        return lax.ppermute(x, "head", [(i, (i + k) % levels) for i in range(levels)])

    def over_ctx(x, mask):
        return lax.ppermute(x, "ctx", [(i, i ^ mask) for i in range(ctx)])

    def slots_of(values, device, part):
        first = device * local_slots + part * run_slots
        return lax.dynamic_slice_in_dim(values, first, run_slots)

    def tables(part):
        frame = jnp.concatenate([slots_of(slot_frame, me, part), slots_of(slot_frame, me ^ 1, part)])
        row = jnp.concatenate([slots_of(slot_row, me, part), slots_of(slot_row, me ^ 1, part)])
        return rope_tables(frame, row)

    turns = [tables(part) for part in range(2)]
    gathered = []
    for part in range(2):
        own = tokens[part * half : (part + 1) * half]
        pieces = [own]
        for k in shifts:
            pieces.append(over_levels(own, k))
        gathered.append(pieces)
    weights = fetch(w_qkv, w_out, levels)
    last, turns, weights = lax.optimization_barrier((gathered[0][-1], turns, weights))
    w_mine, w_rows = weights[0], weights[1].reshape(w_out.shape)
    gathered[0][-1] = last

    projected = []
    for part in range(2):
        mine = gathered[part]
        if part == 1:
            mine[1:], q = lax.optimization_barrier((mine[1:], q))
            projected[0] = (q, pieces)
        theirs = [over_ctx(piece, 1) for piece in mine]
        inputs = ([0] + shifts, mine, theirs, w_mine, *turns[part])
        kv = project("kv", *inputs)
        pieces = [kv]
        for m in range(1, chips):
            pieces.append(over_ctx(kv, 2 * m))
        q = project("q", *inputs)
        projected.append((q, pieces))

    sums = []
    for part in range(2):
        q, pieces = projected[part]
        state = None
        if part == 1:
            state = attend(block_perm, q, None, projected[0][1], [], part, local_slots, False)
            pieces[1:], state = lax.optimization_barrier((pieces[1:], state))
        heads_out = attend(block_perm, q, state, [], pieces, part, local_slots, True)
        theirs = over_ctx(heads_out[half:], 1)
        parts = output_parts(shifts + [0], heads_out, theirs, w_rows)
        arrived = []
        for k, p in zip(shifts, parts):
            arrived.append(over_levels(p, k))
        sums.append([parts[-1]] + arrived)
    return finish(*sums)


def solution(mesh):
    in_specs = (P("ctx", "head"), P(None, None, "head"), P("head", None), P())
    out_specs = P("ctx", "head")

    def body(*args):
        return per_device(mesh.shape["ctx"], mesh.shape["head"], *args)

    return jax.shard_map(
        body, mesh=mesh, in_specs=in_specs, out_specs=out_specs, check_vma=False
    )
```

profile of v0, /device:TPU:0, one launch (start us, length us, event | category | flops | bytes accessed | tf_op | source)
XLA Modules:
  0.0 112.7 jit_solution(5301869761072445915)
XLA Ops:
  1.6 2.6 %collective-permute-start.5 = (bf16[128,768]{1,0:T(8,128)(2,1)S(1)}, bf16[128,768]{1,0:T(8,128)(2,1)S(1)}, u32[]{:S(2)}, u32[]{:S(2)}) collective-permute-start(bf16[128,768]{1,0:T(8,128)(2,1)S(1)} %get-tuple-element.55.refs_2_), channel_id=1, source_target_pairs={{0,1},{1,2},{2,3},{3,0},{4,5},{5,6},{6,7},{7,4},{8,9},{9,10},{10,1... | collective-permute-start | bytes 589832 | tf_op jit(solution)/shard_map/ppermute | solution.py:294
  4.2 2.6 %collective-permute-start.4 = (bf16[128,768]{1,0:T(8,128)(2,1)S(1)}, bf16[128,768]{1,0:T(8,128)(2,1)S(1)}, u32[]{:S(2)}, u32[]{:S(2)}) collective-permute-start(bf16[128,768]{1,0:T(8,128)(2,1)S(1)} %get-tuple-element.55.refs_2_), channel_id=1, source_target_pairs={{0,2},{1,3},{2,0},{3,1},{4,6},{5,7},{6,4},{7,5},{8,10},{9,11},{10,... | collective-permute-start | bytes 589832 | tf_op jit(solution)/shard_map/ppermute | solution.py:294
  10.1 7.3 %fetch.1 = (bf16[3,3072,384]{2,1,0:T(8,128)(2,1)}, bf16[4,192,3072]{2,1,0:T(8,128)(2,1)S(1)}) custom-call(bf16[3,3072,768]{2,1,0:T(8,128)(2,1)} %refs_0_.4, bf16[4,192,3072]{2,1,0:T(8,128)(2,1)} %bitcast.6), custom_call_target="tpu_custom_call" | custom-call | tf_op jit(solution)/shard_map/fetch/pallas_call | solution.py:106
  18.6 1.7 %collective-permute-done.4.refs_3_ = bf16[128,768]{1,0:T(8,128)(2,1)S(1)} collective-permute-done((bf16[128,768]{1,0:T(8,128)(2,1)S(1)}, bf16[128,768]{1,0:T(8,128)(2,1)S(1)}, u32[]{:S(2)}, u32[]{:S(2)}) %collective-permute-start.4) | collective-permute-done | bytes 196640 | tf_op jit(solution)/shard_map/ppermute | solution.py:294
  20.8 5.7 %collective-permute-start.2 = (bf16[128,768]{1,0:T(8,128)(2,1)S(1)}, bf16[128,768]{1,0:T(8,128)(2,1)S(1)}, u32[]{:S(2)}, u32[]{:S(2)}) collective-permute-start(bf16[128,768]{1,0:T(8,128)(2,1)S(1)} %get-tuple-element.56.refs_2_), channel_id=1, source_target_pairs={{0,3},{1,0},{2,1},{3,2},{4,7},{5,4},{6,5},{7,6},{8,11},{9,8},{10,9... | collective-permute-start | bytes 589832 | tf_op jit(solution)/shard_map/ppermute | solution.py:294
  27.1 3.0 %copy-done = bf16[3,3072,384]{2,1,0:T(8,128)(2,1)S(1)} copy-done((bf16[3,3072,384]{2,1,0:T(8,128)(2,1)S(1)}, bf16[3,3072,384]{2,1,0:T(8,128)(2,1)}, u32[]{:S(2)}) %copy-start) | copy-done | bytes 7077912
  31.9 4.7 %collective-permute-done.1.refs_4_ = bf16[128,768]{1,0:T(8,128)(2,1)S(1)} collective-permute-done((bf16[128,768]{1,0:T(8,128)(2,1)S(1)}, bf16[128,768]{1,0:T(8,128)(2,1)S(1)}, u32[]{:S(2)}, u32[]{:S(2)}) %collective-permute-start.1) | collective-permute-done | bytes 196640 | tf_op jit(solution)/shard_map/ppermute | solution.py:294
  36.6 7.8 %collective-permute-done.refs_3_ = bf16[128,768]{1,0:T(8,128)(2,1)S(1)} collective-permute-done((bf16[128,768]{1,0:T(8,128)(2,1)S(1)}, bf16[128,768]{1,0:T(8,128)(2,1)S(1)}, u32[]{:S(2)}, u32[]{:S(2)}) %collective-permute-start) | collective-permute-done | bytes 196640 | tf_op jit(solution)/shard_map/ppermute | solution.py:294
  44.5 1.8 %shard_map.47.refs_2_ = bf16[256,768]{1,0:T(8,128)(2,1)S(1)} custom-call(f32[256,128]{1,0:T(8,128)S(1)} %get-tuple-element.32.refs_0_, f32[256,128]{1,0:T(8,128)S(1)} %get-tuple-element.33.refs_1_, bf16[128,768]{1,0:T(8,128)(2,1)S(1)} %get-tuple-element.55.refs_2_, bf16[128,768]{1,0:T(8,128)(2,1)S(1)} %collective-permute-done.4.refs_3_, ...), custom_call_target="tpu_custom_call" | custom-call | flops 1207959552 | tf_op jit(solution)/shard_map/pallas_call | solution.py:70
  46.3 2.5 %collective-permute-start.12 = (bf16[256,768]{1,0:T(8,128)(2,1)S(1)}, bf16[256,768]{1,0:T(8,128)(2,1)S(1)}, u32[]{:S(2)}, u32[]{:S(2)}) collective-permute-start(bf16[256,768]{1,0:T(8,128)(2,1)S(1)} %shard_map.47.refs_2_), channel_id=1, source_target_pairs={{0,24},{4,28},{8,16},{12,20},{16,8},{20,12},{24,0},{28,4},{1,25},{... | collective-permute-start | bytes 1179656 | tf_op jit(solution)/shard_map/ppermute | solution.py:297
  50.5 1.8 %shard_map.51.refs_3_ = bf16[256,768]{1,0:T(8,128)(2,1)S(1)} custom-call(f32[256,128]{1,0:T(8,128)S(1)} %get-tuple-element.42.refs_0_, f32[256,128]{1,0:T(8,128)S(1)} %get-tuple-element.43.refs_1_, bf16[128,768]{1,0:T(8,128)(2,1)S(1)} %get-tuple-element.56.refs_2_, bf16[128,768]{1,0:T(8,128)(2,1)S(1)} %collective-permute-done.refs_3_, ...), custom_call_target="tpu_custom_call" | custom-call | flops 1207959552 | tf_op jit(solution)/shard_map/pallas_call | solution.py:70
  52.3 2.4 %collective-permute-start.23 = (bf16[256,768]{1,0:T(8,128)(2,1)S(1)}, bf16[256,768]{1,0:T(8,128)(2,1)S(1)}, u32[]{:S(2)}, u32[]{:S(2)}) collective-permute-start(bf16[256,768]{1,0:T(8,128)(2,1)S(1)} %shard_map.51.refs_3_), channel_id=1, source_target_pairs={{0,24},{4,28},{8,16},{12,20},{16,8},{20,12},{24,0},{28,4},{1,25},{... | collective-permute-start | bytes 1179656 | tf_op jit(solution)/shard_map/ppermute | solution.py:297
  55.2 4.1 %collective-permute-done.12.refs_5_ = bf16[256,768]{1,0:T(8,128)(2,1)S(1)} collective-permute-done((bf16[256,768]{1,0:T(8,128)(2,1)S(1)}, bf16[256,768]{1,0:T(8,128)(2,1)S(1)}, u32[]{:S(2)}, u32[]{:S(2)}) %collective-permute-start.12) | collective-permute-done | bytes 393248 | tf_op jit(solution)/shard_map/ppermute | solution.py:297
  60.8 7.0 %collective-permute-done.11.refs_4_ = bf16[256,768]{1,0:T(8,128)(2,1)S(1)} collective-permute-done((bf16[256,768]{1,0:T(8,128)(2,1)S(1)}, bf16[256,768]{1,0:T(8,128)(2,1)S(1)}, u32[]{:S(2)}, u32[]{:S(2)}) %collective-permute-start.11) | collective-permute-done | bytes 393248 | tf_op jit(solution)/shard_map/ppermute | solution.py:297
  67.8 1.7 %shard_map.48.refs_0_ = bf16[256,384]{1,0:T(8,128)(2,1)S(1)} custom-call(s32[32]{0:T(128)S(1)} %copy-done.1, bf16[256,384]{1,0:T(8,128)(2,1)S(1)} %shard_map.46.refs_1_, bf16[256,768]{1,0:T(8,128)(2,1)S(1)} %shard_map.47.refs_2_, bf16[256,768]{1,0:T(8,128)(2,1)S(1)} %collective-permute-done.10.refs_3_, bf16[256,768]{1,0:T(8,128)(2,1)S(1)} %collective-permute-done.11.refs_4_, ...), custom_call_target="tpu_custom_call" | custom-call | flops 805306368 | tf_op jit(solution)/shard_map/pallas_call | solution.py:70
  69.6 1.5 %shard_map.50.refs_1_ = bf16[256,384]{1,0:T(8,128)(2,1)S(1)} custom-call(f32[256,128]{1,0:T(8,128)S(1)} %get-tuple-element.42.refs_0_, f32[256,128]{1,0:T(8,128)S(1)} %get-tuple-element.43.refs_1_, bf16[128,768]{1,0:T(8,128)(2,1)S(1)} %get-tuple-element.56.refs_2_, bf16[128,768]{1,0:T(8,128)(2,1)S(1)} %collective-permute-done.refs_3_, ...), custom_call_target="tpu_custom_call" | custom-call | flops 603979776 | tf_op jit(solution)/shard_map/pallas_call | solution.py:70
  71.1 1.7 %shard_map.52.refs_2_ = f32[256,768]{1,0:T(8,128)S(1)} custom-call(s32[32]{0:T(128)S(1)} %copy-done.1, bf16[256,384]{1,0:T(8,128)(2,1)S(1)} %shard_map.50.refs_1_, bf16[256,768]{1,0:T(8,128)(2,1)S(1)} %shard_map.47.refs_2_, bf16[256,768]{1,0:T(8,128)(2,1)S(1)} %collective-permute-done.10.refs_3_, bf16[256,768]{1,0:T(8,128)(2,1)S(1)} %collective-permute-done.11.refs_4_, ...), custom_call_target="tpu_custom_call" | custom-call | flops 805306368 | tf_op jit(solution)/shard_map/pallas_call | solution.py:70
  73.9 2.3 %collective-permute-done.23.refs_6_ = bf16[256,768]{1,0:T(8,128)(2,1)S(1)} collective-permute-done((bf16[256,768]{1,0:T(8,128)(2,1)S(1)}, bf16[256,768]{1,0:T(8,128)(2,1)S(1)}, u32[]{:S(2)}, u32[]{:S(2)}) %collective-permute-start.23) | collective-permute-done | bytes 393248 | tf_op jit(solution)/shard_map/ppermute | solution.py:297
  76.2 7.9 %collective-permute-done.22.refs_5_ = bf16[256,768]{1,0:T(8,128)(2,1)S(1)} collective-permute-done((bf16[256,768]{1,0:T(8,128)(2,1)S(1)}, bf16[256,768]{1,0:T(8,128)(2,1)S(1)}, u32[]{:S(2)}, u32[]{:S(2)}) %collective-permute-start.22) | collective-permute-done | bytes 393248 | tf_op jit(solution)/shard_map/ppermute | solution.py:297
  84.2 1.6 %shard_map.53.refs_0_ = bf16[256,384]{1,0:T(8,128)(2,1)S(1)} custom-call(s32[32]{0:T(128)S(1)} %copy-done.1, bf16[256,384]{1,0:T(8,128)(2,1)S(1)} %shard_map.50.refs_1_, f32[256,768]{1,0:T(8,128)S(1)} %shard_map.52.refs_2_, bf16[256,768]{1,0:T(8,128)(2,1)S(1)} %shard_map.51.refs_3_, bf16[256,768]{1,0:T(8,128)(2,1)S(1)} %collective-permute-done.21.refs_4_, ...), custom_call_target="tpu_custom_call" | custom-call | flops 805306368 | tf_op jit(solution)/shard_map/pallas_call | solution.py:70
  86.0 3.8 %collective-permute-start.16 = (bf16[128,768]{1,0:T(8,128)(2,1)S(1)}, bf16[128,768]{1,0:T(8,128)(2,1)S(1)}, u32[]{:S(2)}, u32[]{:S(2)}) collective-permute-start(bf16[128,768]{1,0:T(8,128)(2,1)S(1)} %get-tuple-element.41), channel_id=1, source_target_pairs={{0,3},{1,0},{2,1},{3,2},{4,7},{5,4},{6,5},{7,6},{8,11},{9,8},{10,9... | collective-permute-start | bytes 589832 | tf_op jit(solution)/shard_map/ppermute | solution.py:294
  92.3 2.5 %collective-permute-start.27 = (bf16[128,768]{1,0:T(8,128)(2,1)S(1)}, bf16[128,768]{1,0:T(8,128)(2,1)S(1)}, u32[]{:S(2)}, u32[]{:S(2)}) collective-permute-start(bf16[128,768]{1,0:T(8,128)(2,1)S(1)} %get-tuple-element.54), channel_id=1, source_target_pairs={{0,3},{1,0},{2,1},{3,2},{4,7},{5,4},{6,5},{7,6},{8,11},{9,8},{10,9... | collective-permute-start | bytes 589832 | tf_op jit(solution)/shard_map/ppermute | solution.py:294
  95.6 2.4 %collective-permute-done.16.refs_3_ = bf16[128,768]{1,0:T(8,128)(2,1)S(1)} collective-permute-done((bf16[128,768]{1,0:T(8,128)(2,1)S(1)}, bf16[128,768]{1,0:T(8,128)(2,1)S(1)}, u32[]{:S(2)}, u32[]{:S(2)}) %collective-permute-start.16) | collective-permute-done | bytes 196640 | tf_op jit(solution)/shard_map/ppermute | solution.py:294
  98.0 13.8 %collective-permute-done.25.refs_5_ = bf16[128,768]{1,0:T(8,128)(2,1)S(1)} collective-permute-done((bf16[128,768]{1,0:T(8,128)(2,1)S(1)}, bf16[128,768]{1,0:T(8,128)(2,1)S(1)}, u32[]{:S(2)}, u32[]{:S(2)}) %collective-permute-start.25) | collective-permute-done | bytes 196640 | tf_op jit(solution)/shard_map/ppermute | solution.py:294
  (79 shorter events, 18.2 us)
Async XLA Ops:
  1.1 25.5 %collective-permute-start.6 = (bf16[128,768]{1,0:T(8,128)(2,1)S(1)}, bf16[128,768]{1,0:T(8,128)(2,1)S(1)}, u32[]{:S(2)}, u32[]{:S(2)}) collective-permute-start(bf16[128,768]{1,0:T(8,128)(2,1)S(1)} %get-tuple-element.55.refs_2_), channel_id=1, source_target_pairs={{0,4},{4,0},{8,12},{12,8},{16,20},{20,16},{24,28},{28,24},{1,5},{5... | collective-permute-start | bytes 589832 | tf_op jit(solution)/shard_map/ppermute | solution.py:297
  1.6 15.8 %collective-permute-start.5 = (bf16[128,768]{1,0:T(8,128)(2,1)S(1)}, bf16[128,768]{1,0:T(8,128)(2,1)S(1)}, u32[]{:S(2)}, u32[]{:S(2)}) collective-permute-start(bf16[128,768]{1,0:T(8,128)(2,1)S(1)} %get-tuple-element.55.refs_2_), channel_id=1, source_target_pairs={{0,1},{1,2},{2,3},{3,0},{4,5},{5,6},{6,7},{7,4},{8,9},{9,10},{10,1... | collective-permute-start | bytes 589832 | tf_op jit(solution)/shard_map/ppermute | solution.py:294
  4.2 16.1 %collective-permute-start.4 = (bf16[128,768]{1,0:T(8,128)(2,1)S(1)}, bf16[128,768]{1,0:T(8,128)(2,1)S(1)}, u32[]{:S(2)}, u32[]{:S(2)}) collective-permute-start(bf16[128,768]{1,0:T(8,128)(2,1)S(1)} %get-tuple-element.55.refs_2_), channel_id=1, source_target_pairs={{0,2},{1,3},{2,0},{3,1},{4,6},{5,7},{6,4},{7,5},{8,10},{9,11},{10,... | collective-permute-start | bytes 589832 | tf_op jit(solution)/shard_map/ppermute | solution.py:294
  6.8 11.7 %collective-permute-start.3 = (bf16[128,768]{1,0:T(8,128)(2,1)S(1)}, bf16[128,768]{1,0:T(8,128)(2,1)S(1)}, u32[]{:S(2)}, u32[]{:S(2)}) collective-permute-start(bf16[128,768]{1,0:T(8,128)(2,1)S(1)} %get-tuple-element.55.refs_2_), channel_id=1, source_target_pairs={{0,3},{1,0},{2,1},{3,2},{4,7},{5,4},{6,5},{7,6},{8,11},{9,8},{10,9... | collective-permute-start | bytes 589832 | tf_op jit(solution)/shard_map/ppermute | solution.py:294
  17.4 9.1 %collective-permute-start.8 = (bf16[128,768]{1,0:T(8,128)(2,1)S(1)}, bf16[128,768]{1,0:T(8,128)(2,1)S(1)}, u32[]{:S(2)}, u32[]{:S(2)}) collective-permute-start(bf16[128,768]{1,0:T(8,128)(2,1)S(1)} %collective-permute-done.5.refs_4_), channel_id=1, source_target_pairs={{0,4},{4,0},{8,12},{12,8},{16,20},{20,16},{24,28},{28,24},{1,5},{5... | collective-permute-start | bytes 589832 | tf_op jit(solution)/shard_map/ppermute | solution.py:297
  20.3 6.8 %collective-permute-start.7 = (bf16[128,768]{1,0:T(8,128)(2,1)S(1)}, bf16[128,768]{1,0:T(8,128)(2,1)S(1)}, u32[]{:S(2)}, u32[]{:S(2)}) collective-permute-start(bf16[128,768]{1,0:T(8,128)(2,1)S(1)} %collective-permute-done.4.refs_3_), channel_id=1, source_target_pairs={{0,4},{4,0},{8,12},{12,8},{16,20},{20,16},{24,28},{28,24},{1,5},{5... | collective-permute-start | bytes 589832 | tf_op jit(solution)/shard_map/ppermute | solution.py:297
  20.3 6.8 %collective-permute-start.9 = (bf16[128,768]{1,0:T(8,128)(2,1)S(1)}, bf16[128,768]{1,0:T(8,128)(2,1)S(1)}, u32[]{:S(2)}, u32[]{:S(2)}) collective-permute-start(bf16[128,768]{1,0:T(8,128)(2,1)S(1)} %collective-permute-done.3.refs_5_), channel_id=1, source_target_pairs={{0,4},{4,0},{8,12},{12,8},{16,20},{20,16},{24,28},{28,24},{1,5},{5... | collective-permute-start | bytes 589832 | tf_op jit(solution)/shard_map/ppermute | solution.py:297
  20.8 11.1 %collective-permute-start.2 = (bf16[128,768]{1,0:T(8,128)(2,1)S(1)}, bf16[128,768]{1,0:T(8,128)(2,1)S(1)}, u32[]{:S(2)}, u32[]{:S(2)}) collective-permute-start(bf16[128,768]{1,0:T(8,128)(2,1)S(1)} %get-tuple-element.56.refs_2_), channel_id=1, source_target_pairs={{0,3},{1,0},{2,1},{3,2},{4,7},{5,4},{6,5},{7,6},{8,11},{9,8},{10,9... | collective-permute-start | bytes 589832 | tf_op jit(solution)/shard_map/ppermute | solution.py:294
  26.6 10.1 %collective-permute-start.1 = (bf16[128,768]{1,0:T(8,128)(2,1)S(1)}, bf16[128,768]{1,0:T(8,128)(2,1)S(1)}, u32[]{:S(2)}, u32[]{:S(2)}) collective-permute-start(bf16[128,768]{1,0:T(8,128)(2,1)S(1)} %get-tuple-element.56.refs_2_), channel_id=1, source_target_pairs={{0,1},{1,2},{2,3},{3,0},{4,5},{5,6},{6,7},{7,4},{8,9},{9,10},{10,1... | collective-permute-start | bytes 589832 | tf_op jit(solution)/shard_map/ppermute | solution.py:294
  26.6 17.9 %collective-permute-start = (bf16[128,768]{1,0:T(8,128)(2,1)S(1)}, bf16[128,768]{1,0:T(8,128)(2,1)S(1)}, u32[]{:S(2)}, u32[]{:S(2)}) collective-permute-start(bf16[128,768]{1,0:T(8,128)(2,1)S(1)} %get-tuple-element.56.refs_2_), channel_id=1, source_target_pairs={{0,2},{1,3},{2,0},{3,1},{4,6},{5,7},{6,4},{7,5},{8,10},{9,11},{10,... | collective-permute-start | bytes 589832 | tf_op jit(solution)/shard_map/ppermute | solution.py:294
  27.1 22.2 %collective-permute-start.17 = (bf16[128,768]{1,0:T(8,128)(2,1)S(1)}, bf16[128,768]{1,0:T(8,128)(2,1)S(1)}, u32[]{:S(2)}, u32[]{:S(2)}) collective-permute-start(bf16[128,768]{1,0:T(8,128)(2,1)S(1)} %get-tuple-element.56.refs_2_), channel_id=1, source_target_pairs={{0,4},{4,0},{8,12},{12,8},{16,20},{20,16},{24,28},{28,24},{1,5},{5... | collective-permute-start | bytes 589832 | tf_op jit(solution)/shard_map/ppermute | solution.py:297
  44.5 5.4 %collective-permute-start.18 = (bf16[128,768]{1,0:T(8,128)(2,1)S(1)}, bf16[128,768]{1,0:T(8,128)(2,1)S(1)}, u32[]{:S(2)}, u32[]{:S(2)}) collective-permute-start(bf16[128,768]{1,0:T(8,128)(2,1)S(1)} %collective-permute-done.refs_3_), channel_id=1, source_target_pairs={{0,4},{4,0},{8,12},{12,8},{16,20},{20,16},{24,28},{28,24},{1,5},{5... | collective-permute-start | bytes 589832 | tf_op jit(solution)/shard_map/ppermute | solution.py:297
  46.3 13.0 %collective-permute-start.12 = (bf16[256,768]{1,0:T(8,128)(2,1)S(1)}, bf16[256,768]{1,0:T(8,128)(2,1)S(1)}, u32[]{:S(2)}, u32[]{:S(2)}) collective-permute-start(bf16[256,768]{1,0:T(8,128)(2,1)S(1)} %shard_map.47.refs_2_), channel_id=1, source_target_pairs={{0,24},{4,28},{8,16},{12,20},{16,8},{20,12},{24,0},{28,4},{1,25},{... | collective-permute-start | bytes 1179656 | tf_op jit(solution)/shard_map/ppermute | solution.py:297
  49.3 18.4 %collective-permute-start.11 = (bf16[256,768]{1,0:T(8,128)(2,1)S(1)}, bf16[256,768]{1,0:T(8,128)(2,1)S(1)}, u32[]{:S(2)}, u32[]{:S(2)}) collective-permute-start(bf16[256,768]{1,0:T(8,128)(2,1)S(1)} %shard_map.47.refs_2_), channel_id=1, source_target_pairs={{0,16},{4,20},{8,24},{12,28},{16,0},{20,4},{24,8},{28,12},{1,17},{... | collective-permute-start | bytes 1179656 | tf_op jit(solution)/shard_map/ppermute | solution.py:297
  49.8 17.9 %collective-permute-start.10 = (bf16[256,768]{1,0:T(8,128)(2,1)S(1)}, bf16[256,768]{1,0:T(8,128)(2,1)S(1)}, u32[]{:S(2)}, u32[]{:S(2)}) collective-permute-start(bf16[256,768]{1,0:T(8,128)(2,1)S(1)} %shard_map.47.refs_2_), channel_id=1, source_target_pairs={{0,8},{4,12},{8,0},{12,4},{16,24},{20,28},{24,16},{28,20},{1,9},{5... | collective-permute-start | bytes 1179656 | tf_op jit(solution)/shard_map/ppermute | solution.py:297
  52.3 23.9 %collective-permute-start.23 = (bf16[256,768]{1,0:T(8,128)(2,1)S(1)}, bf16[256,768]{1,0:T(8,128)(2,1)S(1)}, u32[]{:S(2)}, u32[]{:S(2)}) collective-permute-start(bf16[256,768]{1,0:T(8,128)(2,1)S(1)} %shard_map.51.refs_3_), channel_id=1, source_target_pairs={{0,24},{4,28},{8,16},{12,20},{16,8},{20,12},{24,0},{28,4},{1,25},{... | collective-permute-start | bytes 1179656 | tf_op jit(solution)/shard_map/ppermute | solution.py:297
  54.7 29.4 %collective-permute-start.22 = (bf16[256,768]{1,0:T(8,128)(2,1)S(1)}, bf16[256,768]{1,0:T(8,128)(2,1)S(1)}, u32[]{:S(2)}, u32[]{:S(2)}) collective-permute-start(bf16[256,768]{1,0:T(8,128)(2,1)S(1)} %shard_map.51.refs_3_), channel_id=1, source_target_pairs={{0,16},{4,20},{8,24},{12,28},{16,0},{20,4},{24,8},{28,12},{1,17},{... | collective-permute-start | bytes 1179656 | tf_op jit(solution)/shard_map/ppermute | solution.py:297
  59.3 24.9 %collective-permute-start.21 = (bf16[256,768]{1,0:T(8,128)(2,1)S(1)}, bf16[256,768]{1,0:T(8,128)(2,1)S(1)}, u32[]{:S(2)}, u32[]{:S(2)}) collective-permute-start(bf16[256,768]{1,0:T(8,128)(2,1)S(1)} %shard_map.51.refs_3_), channel_id=1, source_target_pairs={{0,8},{4,12},{8,0},{12,4},{16,24},{20,28},{24,16},{28,20},{1,9},{5... | collective-permute-start | bytes 1179656 | tf_op jit(solution)/shard_map/ppermute | solution.py:297
  73.8 18.5 %collective-permute-start.14 = (bf16[128,768]{1,0:T(8,128)(2,1)S(1)}, bf16[128,768]{1,0:T(8,128)(2,1)S(1)}, u32[]{:S(2)}, u32[]{:S(2)}) collective-permute-start(bf16[128,768]{1,0:T(8,128)(2,1)S(1)} %get-tuple-element.39), channel_id=1, source_target_pairs={{0,2},{1,3},{2,0},{3,1},{4,6},{5,7},{6,4},{7,5},{8,10},{9,11},{10,... | collective-permute-start | bytes 589832 | tf_op jit(solution)/shard_map/ppermute | solution.py:294
  85.9 9.7 %collective-permute-start.15 = (bf16[128,768]{1,0:T(8,128)(2,1)S(1)}, bf16[128,768]{1,0:T(8,128)(2,1)S(1)}, u32[]{:S(2)}, u32[]{:S(2)}) collective-permute-start(bf16[128,768]{1,0:T(8,128)(2,1)S(1)} %get-tuple-element.40), channel_id=1, source_target_pairs={{0,1},{1,2},{2,3},{3,0},{4,5},{5,6},{6,7},{7,4},{8,9},{9,10},{10,1... | collective-permute-start | bytes 589832 | tf_op jit(solution)/shard_map/ppermute | solution.py:294
  86.0 12.0 %collective-permute-start.16 = (bf16[128,768]{1,0:T(8,128)(2,1)S(1)}, bf16[128,768]{1,0:T(8,128)(2,1)S(1)}, u32[]{:S(2)}, u32[]{:S(2)}) collective-permute-start(bf16[128,768]{1,0:T(8,128)(2,1)S(1)} %get-tuple-element.41), channel_id=1, source_target_pairs={{0,3},{1,0},{2,1},{3,2},{4,7},{5,4},{6,5},{7,6},{8,11},{9,8},{10,9... | collective-permute-start | bytes 589832 | tf_op jit(solution)/shard_map/ppermute | solution.py:294
  90.8 21.0 %collective-permute-start.25 = (bf16[128,768]{1,0:T(8,128)(2,1)S(1)}, bf16[128,768]{1,0:T(8,128)(2,1)S(1)}, u32[]{:S(2)}, u32[]{:S(2)}) collective-permute-start(bf16[128,768]{1,0:T(8,128)(2,1)S(1)} %get-tuple-element.52), channel_id=1, source_target_pairs={{0,2},{1,3},{2,0},{3,1},{4,6},{5,7},{6,4},{7,5},{8,10},{9,11},{10,... | collective-permute-start | bytes 589832 | tf_op jit(solution)/shard_map/ppermute | solution.py:294
  90.9 20.9 %collective-permute-start.26 = (bf16[128,768]{1,0:T(8,128)(2,1)S(1)}, bf16[128,768]{1,0:T(8,128)(2,1)S(1)}, u32[]{:S(2)}, u32[]{:S(2)}) collective-permute-start(bf16[128,768]{1,0:T(8,128)(2,1)S(1)} %get-tuple-element.53), channel_id=1, source_target_pairs={{0,1},{1,2},{2,3},{3,0},{4,5},{5,6},{6,7},{7,4},{8,9},{9,10},{10,1... | collective-permute-start | bytes 589832 | tf_op jit(solution)/shard_map/ppermute | solution.py:294
  92.3 19.5 %collective-permute-start.27 = (bf16[128,768]{1,0:T(8,128)(2,1)S(1)}, bf16[128,768]{1,0:T(8,128)(2,1)S(1)}, u32[]{:S(2)}, u32[]{:S(2)}) collective-permute-start(bf16[128,768]{1,0:T(8,128)(2,1)S(1)} %get-tuple-element.54), channel_id=1, source_target_pairs={{0,3},{1,0},{2,1},{3,2},{4,7},{5,4},{6,5},{7,6},{8,11},{9,8},{10,9... | collective-permute-start | bytes 589832 | tf_op jit(solution)/shard_map/ppermute | solution.py:294
  (9 other events, 105.2 us)
where the time goes:
time: 114 us; the launch traced here: 113 us
  waiting for transfers between devices  53.1 us (47%)
  starting transfers between devices  30.5 us (27%)
  Pallas kernels  21.9 us (19%)
  local copies, waits for them, and re-layouts  4.97 us (4%)
  other arithmetic  2.05 us (2%)
    ppermute x12, waiting for transfers between devices, over_levels(): lax.ppermute(x, 'head', [(i, (i + k) % levels) for i in range(levels)])  31.5 us
    ppermute x16, waiting for transfers between devices, over_ctx(): return lax.ppermute(x, 'ctx', [(i, i ^ mask) for i in range(ctx)])  21.6 us
    ppermute x12, starting transfers between devices, over_levels(): lax.ppermute(x, 'head', [(i, (i + k) % levels) for i in range(levels)])  20.7 us
    pallas_call x10, Pallas kernels, vmem_call(): pl.pallas_call(kernel, in_specs=[pl.BlockSpec(memory_space=pltpu.SMEM)] *...  14.6 us
    ppermute x16, starting transfers between devices, over_ctx(): return lax.ppermute(x, 'ctx', [(i, i ^ mask) for i in range(ctx)])  9.71 us
    pallas_call x1, Pallas kernels, fetch(): pl.pallas_call(functools.partial(fetch_kernel, (True, False)), in_specs=[...  7.32 us
    unnamed x10, local copies, waits for them, and re-layouts  3.02 us
  transfers between devices with their start and end apart: 28, of which 13 were waited for; matrix products, arithmetic and copies ran while one was open for 3% of the time, Pallas kernels for 19%

commit v1 on v0

--- a/solution.py
+++ b/solution.py
@@ -80,38 +80,31 @@
     )(*smem, *after, *inputs)
 
 
-def fetch_kernel(cuts, *refs):
-    count = len(cuts)
-    sources, targets, sems = refs[:count], refs[count : 2 * count], refs[2 * count]
+def fetch_kernel(w_ref, out_ref, sems):
+    width = out_ref.shape[2]
     core = lax.axis_index("ctx") % CORES
-    copies = []
-    for source, target, cut in zip(sources, targets, cuts):
-        for at in range(target.shape[0]):
-            view = source.at[at]
-            if cut:
-                width = target.shape[-1]
-                cols = pl.ds(pl.multiple_of(core * width, width), width)
-                view = source.at[at, :, cols]
-            copies.append(pltpu.make_async_copy(view, target.at[at], sems.at[len(copies)]))
+    cols = pl.ds(pl.multiple_of(core * width, width), width)
+    copies = [
+        pltpu.make_async_copy(w_ref.at[at, :, cols], out_ref.at[at], sems.at[at])
+        for at in range(out_ref.shape[0])
+    ]
     for copy in copies:
         copy.start()
     for copy in copies:
         copy.wait()
 
 
-def fetch(w_qkv, w_out, pieces):
+def fetch(w_qkv):
     three, feats, cols = w_qkv.shape
-    shapes = [(three, feats, cols // CORES), (pieces, w_out.shape[0] // pieces, w_out.shape[1])]
-    any_space = pl.BlockSpec(memory_space=pltpu.MemorySpace.HBM)
     return pl.pallas_call(
-        functools.partial(fetch_kernel, (True, False)),
-        in_specs=[any_space] * 2,
-        out_specs=[pl.BlockSpec(memory_space=pltpu.VMEM)] * 2,
-        out_shape=[jax.ShapeDtypeStruct(shape, jnp.bfloat16) for shape in shapes],
-        scratch_shapes=[pltpu.SemaphoreType.DMA((three + pieces,))],
+        fetch_kernel,
+        in_specs=[pl.BlockSpec(memory_space=pltpu.MemorySpace.HBM)],
+        out_specs=pl.BlockSpec(memory_space=pltpu.VMEM),
+        out_shape=jax.ShapeDtypeStruct((three, feats, cols // CORES), jnp.bfloat16),
+        scratch_shapes=[pltpu.SemaphoreType.DMA((three,))],
         compiler_params=pltpu.CompilerParams(vmem_limit_bytes=46 << 20),
         name="fetch",
-    )(w_qkv, w_out.reshape(shapes[1]))
+    )(w_qkv)
 
 
 def project_kernel(pieces, heads, shifts, kind, cos_ref, sin_ref, *refs):
@@ -125,7 +118,7 @@
     def product(j):
         total = None
         for i, k in enumerate(shifts):
-            block = lax.rem(level - k + pieces, pieces)
+            block = level ^ k
             at = pl.ds(pl.multiple_of(block * feats, feats), feats)
             x = jnp.concatenate([mine[i][...], theirs[i][...]], axis=0)
             dot = jnp.dot(x, w_ref[j, at, :], preferred_element_type=jnp.float32)
@@ -155,7 +148,9 @@
     )
 
 
-def attend_kernel(carried, final, free, masked, heads, part, local_slots, perm_ref, q_ref, *refs):
+def attend_kernel(
+    carried, sides, final, free, masked, heads, part, local_slots, perm_ref, q_ref, *refs
+):
     state_ref = refs[0] if carried else None
     kv = refs[carried : carried + free + masked]
     out_ref = refs[-1]
@@ -171,8 +166,9 @@
     for h in range(heads):
         cols = pl.ds(h * HD, HD)
         wide_cols = pl.ds(2 * h * HD, 2 * HD)
-        for r in range(2):
+        for r in sides:
             window = pl.ds(r * rows, rows)
+            target = window if len(sides) == 2 else slice(None)
             q = q_ref[window, cols]
             if carried:
                 acc = state_ref[window, wide_cols]
@@ -198,28 +194,29 @@
                 wide = jnp.concatenate([values, jnp.ones_like(values)], axis=1)
                 acc += jnp.dot(weights, wide, preferred_element_type=jnp.float32)
             if final:
-                out_ref[window, cols] = (acc[:, :HD] / acc[:, HD:]).astype(jnp.bfloat16)
+                out_ref[target, cols] = (acc[:, :HD] / acc[:, HD:]).astype(jnp.bfloat16)
             else:
-                out_ref[window, wide_cols] = acc
-
-
-def attend(block_perm, q, state, free, masked, part, local_slots, final):
+                out_ref[target, wide_cols] = acc
+
+
+def attend(block_perm, q, state, free, masked, part, local_slots, sides, final):
     rows2, width = q.shape
     heads = width // HD
     keys = sum(p.shape[0] for p in free + masked)
     carried = 0 if state is None else 1
+    out_rows = rows2 * len(sides) // 2
     if final:
-        out = jax.ShapeDtypeStruct((rows2, width), jnp.bfloat16)
+        out = jax.ShapeDtypeStruct((out_rows, width), jnp.bfloat16)
     else:
-        out = jax.ShapeDtypeStruct((rows2, 2 * width), jnp.float32)
+        out = jax.ShapeDtypeStruct((out_rows, 2 * width), jnp.float32)
     return vmem_call(
         functools.partial(
-            attend_kernel, carried, final, len(free), len(masked), heads, part, local_slots
+            attend_kernel, carried, sides, final, len(free), len(masked), heads, part, local_slots
         ),
         [q] + ([state] if carried else []) + free + masked,
         [out],
         smem=[block_perm],
-        flops=8 * rows2 * keys * width,
+        flops=8 * out_rows * keys * width,
     )
 
 
@@ -235,7 +232,7 @@
     theirs = theirs_ref[...]
     span = w_ref.shape[1] // levels
     for i, k in enumerate(shifts):
-        block = lax.rem(level + k, levels)
+        block = level ^ k
         cols = pl.ds(pl.multiple_of(block * span, span), span)
         part = jnp.dot(mine, w_ref[mine_at, cols], preferred_element_type=jnp.float32)
         part += jnp.dot(theirs, w_ref[theirs_at, cols], preferred_element_type=jnp.float32)
@@ -288,10 +285,10 @@
     slot_frame = block_perm // frame_rows
     slot_row = block_perm % frame_rows
 
-    shifts = sorted(range(1, levels), key=lambda k: (-min(k, levels - k), k))
+    shifts = list(range(levels - 1, 0, -1))
 
     def over_levels(x, k):
-        return lax.ppermute(x, "head", [(i, (i + k) % levels) for i in range(levels)])
+        return lax.ppermute(x, "head", [(i, i ^ k) for i in range(levels)])
 
     def over_ctx(x, mask):
         return lax.ppermute(x, "ctx", [(i, i ^ mask) for i in range(ctx)])
@@ -307,15 +304,18 @@
 
     turns = [tables(part) for part in range(2)]
     gathered = []
+    held = None
     for part in range(2):
+        if held is not None:
+            tokens, gathered[0][1:] = lax.optimization_barrier((tokens, held))
         own = tokens[part * half : (part + 1) * half]
         pieces = [own]
         for k in shifts:
             pieces.append(over_levels(own, k))
+        held = pieces[1:]
         gathered.append(pieces)
-    weights = fetch(w_qkv, w_out, levels)
-    last, turns, weights = lax.optimization_barrier((gathered[0][-1], turns, weights))
-    w_mine, w_rows = weights[0], weights[1].reshape(w_out.shape)
+    w_mine = fetch(w_qkv)
+    last, turns, w_mine = lax.optimization_barrier((gathered[0][-1], turns, w_mine))
     gathered[0][-1] = last
 
     projected = []
@@ -324,7 +324,9 @@
         if part == 1:
             mine[1:], q = lax.optimization_barrier((mine[1:], q))
             projected[0] = (q, pieces)
-        theirs = [over_ctx(piece, 1) for piece in mine]
+        theirs = []
+        for piece in mine:
+            theirs.append(over_ctx(piece, 1))
         inputs = ([0] + shifts, mine, theirs, w_mine, *turns[part])
         kv = project("kv", *inputs)
         pieces = [kv]
@@ -332,17 +334,20 @@
             pieces.append(over_ctx(kv, 2 * m))
         q = project("q", *inputs)
         projected.append((q, pieces))
-
     sums = []
     for part in range(2):
         q, pieces = projected[part]
         state = None
         if part == 1:
-            state = attend(block_perm, q, None, projected[0][1], [], part, local_slots, False)
+            state = attend(block_perm, q, None, projected[0][1], [], part, local_slots, (0, 1), False)
             pieces[1:], state = lax.optimization_barrier((pieces[1:], state))
-        heads_out = attend(block_perm, q, state, [], pieces, part, local_slots, True)
-        theirs = over_ctx(heads_out[half:], 1)
-        parts = output_parts(shifts + [0], heads_out, theirs, w_rows)
+        both = []
+        for side in (1, 0):
+            both.append(attend(block_perm, q, state, [], pieces, part, local_slots, (side,), True))
+            if side == 1:
+                theirs = over_ctx(both[0], 1)
+        heads_out = both[1]
+        parts = output_parts(shifts + [0], heads_out, theirs, w_out)
         arrived = []
         for k, p in zip(shifts, parts):
             arrived.append(over_levels(p, k))

time: 114 us -> 118 us (1.035)
  starting transfers between devices: 30.5 us -> 33.6 us
  local copies, waits for them, and re-layouts: 4.97 us -> 7.71 us
  Pallas kernels: 21.9 us -> 19.7 us
  waiting for transfers between devices: 53.1 us -> 54.6 us
    ppermute x12, waiting for transfers between devices: 31.5 us -> 36.6 us  [over_levels(): return lax.ppermute(x, 'head', [(i, i ^ k) for i in range(levels)])]
    pallas_call x1, Pallas kernels: 7.32 us -> 3.16 us  [fetch(): pl.pallas_call(fetch_kernel, in_specs=[pl.BlockSpec(memory_space=pltpu.Me...]
    ppermute x16, waiting for transfers between devices: 21.6 us -> 18 us  [over_ctx(): return lax.ppermute(x, 'ctx', [(i, i ^ mask) for i in range(ctx)])]
    ppermute x12, starting transfers between devices: 20.7 us -> 23.8 us  [over_levels(): return lax.ppermute(x, 'head', [(i, i ^ k) for i in range(levels)])]
    unnamed x10 -> x18, local copies, waits for them, and re-layouts: 3.02 us -> 5.88 us
    pallas_call x10 -> x12, Pallas kernels: 14.6 us -> 16.5 us  [vmem_call(): pl.pallas_call(kernel, in_specs=[pl.BlockSpec(memory_space=pltpu.SMEM)] *...]
  transfers between devices with their start and end apart: 28 -> 28, of which waited for: 13 -> 12; matrix products, arithmetic and copies ran while one was open for 3% -> 3% of each run, Pallas kernels for 19% -> 16%
where the time goes in v1:
time: 118 us
  waiting for transfers between devices  54.6 us (46%)
  starting transfers between devices  33.6 us (28%)
  Pallas kernels  19.7 us (17%)
  local copies, waits for them, and re-layouts  7.71 us (7%)
  other arithmetic  2.05 us (2%)
    ppermute x12, waiting for transfers between devices, over_levels(): return lax.ppermute(x, 'head', [(i, i ^ k) for i in range(levels)])  36.6 us
    ppermute x12, starting transfers between devices, over_levels(): return lax.ppermute(x, 'head', [(i, i ^ k) for i in range(levels)])  23.8 us
    ppermute x16, waiting for transfers between devices, over_ctx(): return lax.ppermute(x, 'ctx', [(i, i ^ mask) for i in range(ctx)])  18 us
    pallas_call x12, Pallas kernels, vmem_call(): pl.pallas_call(kernel, in_specs=[pl.BlockSpec(memory_space=pltpu.SMEM)] *...  16.5 us
    ppermute x16, starting transfers between devices, over_ctx(): return lax.ppermute(x, 'ctx', [(i, i ^ mask) for i in range(ctx)])  9.77 us
    unnamed x18, local copies, waits for them, and re-layouts  5.88 us
    pallas_call x1, Pallas kernels, fetch(): pl.pallas_call(fetch_kernel, in_specs=[pl.BlockSpec(memory_space=pltpu.Me...  3.16 us
  transfers between devices with their start and end apart: 28, of which 12 were waited for; matrix products, arithmetic and copies ran while one was open for 3% of the time, Pallas kernels for 16%

profile of v1, /device:TPU:0, one launch (start us, length us, event | category | flops | bytes accessed | tf_op | source)
XLA Modules:
  0.0 117.8 jit_solution(4329362650424961567)
XLA Ops:
  1.5 2.6 %collective-permute-start.2 = (bf16[128,768]{1,0:T(8,128)(2,1)S(1)}, bf16[128,768]{1,0:T(8,128)(2,1)S(1)}, u32[]{:S(2)}, u32[]{:S(2)}) collective-permute-start(bf16[128,768]{1,0:T(8,128)(2,1)S(1)} %slice.6.refs_2_), channel_id=1, source_target_pairs={{0,1},{1,0},{2,3},{3,2},{4,5},{5,4},{6,7},{7,6},{8,9},{9,8},{10,11... | collective-permute-start | bytes 589832 | tf_op jit(solution)/shard_map/ppermute | solution.py:291
  4.1 2.6 %collective-permute-start.1 = (bf16[128,768]{1,0:T(8,128)(2,1)S(1)}, bf16[128,768]{1,0:T(8,128)(2,1)S(1)}, u32[]{:S(2)}, u32[]{:S(2)}) collective-permute-start(bf16[128,768]{1,0:T(8,128)(2,1)S(1)} %slice.6.refs_2_), channel_id=1, source_target_pairs={{0,2},{1,3},{2,0},{3,1},{4,6},{5,7},{6,4},{7,5},{8,10},{9,11},{10,... | collective-permute-start | bytes 589832 | tf_op jit(solution)/shard_map/ppermute | solution.py:291
  8.5 3.2 %fetch.1.refs_10_ = bf16[3,3072,384]{2,1,0:T(8,128)(2,1)S(1)} custom-call(bf16[3,3072,768]{2,1,0:T(8,128)(2,1)} %w_ref.1), custom_call_target="tpu_custom_call" | custom-call | tf_op jit(solution)/shard_map/fetch/pallas_call | solution.py:99
  11.7 2.8 %copy-done = bf16[3,3072,384]{2,1,0:T(8,128)(2,1)} copy-done((bf16[3,3072,384]{2,1,0:T(8,128)(2,1)}, bf16[3,3072,384]{2,1,0:T(8,128)(2,1)S(1)}, u32[]{:S(2)}) %copy-start) | copy-done | bytes 7077912
  14.7 6.6 %collective-permute-done.1.refs_4_ = bf16[128,768]{1,0:T(8,128)(2,1)S(1)} collective-permute-done((bf16[128,768]{1,0:T(8,128)(2,1)S(1)}, bf16[128,768]{1,0:T(8,128)(2,1)S(1)}, u32[]{:S(2)}, u32[]{:S(2)}) %collective-permute-start.1) | collective-permute-done | bytes 196640 | tf_op jit(solution)/shard_map/ppermute | solution.py:291
  23.0 4.0 %collective-permute-start.5 = (bf16[128,768]{1,0:T(8,128)(2,1)S(1)}, bf16[128,768]{1,0:T(8,128)(2,1)S(1)}, u32[]{:S(2)}, u32[]{:S(2)}) collective-permute-start(bf16[128,768]{1,0:T(8,128)(2,1)S(1)} %slice.7.refs_2_), channel_id=1, source_target_pairs={{0,1},{1,0},{2,3},{3,2},{4,5},{5,4},{6,7},{7,6},{8,9},{9,8},{10,11... | collective-permute-start | bytes 589832 | tf_op jit(solution)/shard_map/ppermute | solution.py:291
  29.6 3.0 %copy-done.1 = bf16[3,3072,384]{2,1,0:T(8,128)(2,1)S(1)} copy-done((bf16[3,3072,384]{2,1,0:T(8,128)(2,1)S(1)}, bf16[3,3072,384]{2,1,0:T(8,128)(2,1)}, u32[]{:S(2)}) %copy-start.1) | copy-done | bytes 7077912
  34.1 2.2 %collective-permute-done.5.refs_5_ = bf16[128,768]{1,0:T(8,128)(2,1)S(1)} collective-permute-done((bf16[128,768]{1,0:T(8,128)(2,1)S(1)}, bf16[128,768]{1,0:T(8,128)(2,1)S(1)}, u32[]{:S(2)}, u32[]{:S(2)}) %collective-permute-start.5) | collective-permute-done | bytes 196640 | tf_op jit(solution)/shard_map/ppermute | solution.py:291
  36.3 7.9 %collective-permute-done.4.refs_4_ = bf16[128,768]{1,0:T(8,128)(2,1)S(1)} collective-permute-done((bf16[128,768]{1,0:T(8,128)(2,1)S(1)}, bf16[128,768]{1,0:T(8,128)(2,1)S(1)}, u32[]{:S(2)}, u32[]{:S(2)}) %collective-permute-start.4) | collective-permute-done | bytes 196640 | tf_op jit(solution)/shard_map/ppermute | solution.py:291
  44.2 1.8 %shard_map.47.refs_2_ = bf16[256,768]{1,0:T(8,128)(2,1)S(1)} custom-call(f32[256,128]{1,0:T(8,128)S(1)} %get-tuple-element.33.refs_0_, f32[256,128]{1,0:T(8,128)S(1)} %get-tuple-element.34.refs_1_, bf16[128,768]{1,0:T(8,128)(2,1)S(1)} %slice.6.refs_2_, bf16[128,768]{1,0:T(8,128)(2,1)S(1)} %collective-permute-done.refs_3_, ...), custom_call_target="tpu_custom_call" | custom-call | flops 1207959552 | tf_op jit(solution)/shard_map/pallas_call | solution.py:70
  46.0 2.5 %collective-permute-start.12 = (bf16[256,768]{1,0:T(8,128)(2,1)S(1)}, bf16[256,768]{1,0:T(8,128)(2,1)S(1)}, u32[]{:S(2)}, u32[]{:S(2)}) collective-permute-start(bf16[256,768]{1,0:T(8,128)(2,1)S(1)} %shard_map.47.refs_2_), channel_id=1, source_target_pairs={{0,24},{4,28},{8,16},{12,20},{16,8},{20,12},{24,0},{28,4},{1,25},{... | collective-permute-start | bytes 1179656 | tf_op jit(solution)/shard_map/ppermute | solution.py:294
  50.3 1.8 %shard_map.52.refs_3_ = bf16[256,768]{1,0:T(8,128)(2,1)S(1)} custom-call(f32[256,128]{1,0:T(8,128)S(1)} %get-tuple-element.44.refs_0_, f32[256,128]{1,0:T(8,128)S(1)} %get-tuple-element.45.refs_1_, bf16[128,768]{1,0:T(8,128)(2,1)S(1)} %slice.7.refs_2_, bf16[128,768]{1,0:T(8,128)(2,1)S(1)} %collective-permute-done.3.refs_3_, ...), custom_call_target="tpu_custom_call" | custom-call | flops 1207959552 | tf_op jit(solution)/shard_map/pallas_call | solution.py:70
  52.1 2.4 %collective-permute-start.23 = (bf16[256,768]{1,0:T(8,128)(2,1)S(1)}, bf16[256,768]{1,0:T(8,128)(2,1)S(1)}, u32[]{:S(2)}, u32[]{:S(2)}) collective-permute-start(bf16[256,768]{1,0:T(8,128)(2,1)S(1)} %shard_map.52.refs_3_), channel_id=1, source_target_pairs={{0,24},{4,28},{8,16},{12,20},{16,8},{20,12},{24,0},{28,4},{1,25},{... | collective-permute-start | bytes 1179656 | tf_op jit(solution)/shard_map/ppermute | solution.py:294
  54.9 4.1 %collective-permute-done.12.refs_5_ = bf16[256,768]{1,0:T(8,128)(2,1)S(1)} collective-permute-done((bf16[256,768]{1,0:T(8,128)(2,1)S(1)}, bf16[256,768]{1,0:T(8,128)(2,1)S(1)}, u32[]{:S(2)}, u32[]{:S(2)}) %collective-permute-start.12) | collective-permute-done | bytes 393248 | tf_op jit(solution)/shard_map/ppermute | solution.py:294
  60.5 7.0 %collective-permute-done.11.refs_4_ = bf16[256,768]{1,0:T(8,128)(2,1)S(1)} collective-permute-done((bf16[256,768]{1,0:T(8,128)(2,1)S(1)}, bf16[256,768]{1,0:T(8,128)(2,1)S(1)}, u32[]{:S(2)}, u32[]{:S(2)}) %collective-permute-start.11) | collective-permute-done | bytes 393248 | tf_op jit(solution)/shard_map/ppermute | solution.py:294
  72.8 2.5 %collective-permute-start.14 = (bf16[128,768]{1,0:T(8,128)(2,1)S(1)}, bf16[128,768]{1,0:T(8,128)(2,1)S(1)}, u32[]{:S(2)}, u32[]{:S(2)}) collective-permute-start(bf16[128,768]{1,0:T(8,128)(2,1)S(1)} %get-tuple-element.41), channel_id=1, source_target_pairs={{0,3},{1,2},{2,1},{3,0},{4,7},{5,6},{6,5},{7,4},{8,11},{9,10},{10,... | collective-permute-start | bytes 589832 | tf_op jit(solution)/shard_map/ppermute | solution.py:291
  75.3 1.9 %shard_map.53.refs_2_ = f32[256,768]{1,0:T(8,128)S(1)} custom-call(s32[32]{0:T(128)S(1)} %copy-done.2, bf16[256,384]{1,0:T(8,128)(2,1)S(1)} %shard_map.51.refs_1_, bf16[256,768]{1,0:T(8,128)(2,1)S(1)} %shard_map.47.refs_2_, bf16[256,768]{1,0:T(8,128)(2,1)S(1)} %collective-permute-done.10.refs_3_, bf16[256,768]{1,0:T(8,128)(2,1)S(1)} %collective-permute-done.11.refs_4_, ...), custom_call_target="tpu_custom_call" | custom-call | flops 805306368 | tf_op jit(solution)/shard_map/pallas_call | solution.py:70
  77.2 6.6 %collective-permute-done.22.refs_5_ = bf16[256,768]{1,0:T(8,128)(2,1)S(1)} collective-permute-done((bf16[256,768]{1,0:T(8,128)(2,1)S(1)}, bf16[256,768]{1,0:T(8,128)(2,1)S(1)}, u32[]{:S(2)}, u32[]{:S(2)}) %collective-permute-start.22) | collective-permute-done | bytes 393248 | tf_op jit(solution)/shard_map/ppermute | solution.py:294
  85.2 5.0 %collective-permute-start.15 = (bf16[128,768]{1,0:T(8,128)(2,1)S(1)}, bf16[128,768]{1,0:T(8,128)(2,1)S(1)}, u32[]{:S(2)}, u32[]{:S(2)}) collective-permute-start(bf16[128,768]{1,0:T(8,128)(2,1)S(1)} %get-tuple-element.42), channel_id=1, source_target_pairs={{0,2},{1,3},{2,0},{3,1},{4,6},{5,7},{6,4},{7,5},{8,10},{9,11},{10,... | collective-permute-start | bytes 589832 | tf_op jit(solution)/shard_map/ppermute | solution.py:291
  92.6 1.6 %collective-permute-start.25 = (bf16[128,768]{1,0:T(8,128)(2,1)S(1)}, bf16[128,768]{1,0:T(8,128)(2,1)S(1)}, u32[]{:S(2)}, u32[]{:S(2)}) collective-permute-start(bf16[128,768]{1,0:T(8,128)(2,1)S(1)} %get-tuple-element.54), channel_id=1, source_target_pairs={{0,3},{1,2},{2,1},{3,0},{4,7},{5,6},{6,5},{7,4},{8,11},{9,10},{10,... | collective-permute-start | bytes 589832 | tf_op jit(solution)/shard_map/ppermute | solution.py:291
  94.2 2.0 %collective-permute-start.26 = (bf16[128,768]{1,0:T(8,128)(2,1)S(1)}, bf16[128,768]{1,0:T(8,128)(2,1)S(1)}, u32[]{:S(2)}, u32[]{:S(2)}) collective-permute-start(bf16[128,768]{1,0:T(8,128)(2,1)S(1)} %get-tuple-element.55), channel_id=1, source_target_pairs={{0,2},{1,3},{2,0},{3,1},{4,6},{5,7},{6,4},{7,5},{8,10},{9,11},{10,... | collective-permute-start | bytes 589832 | tf_op jit(solution)/shard_map/ppermute | solution.py:291
  97.0 3.3 %collective-permute-done.15.refs_2_ = bf16[128,768]{1,0:T(8,128)(2,1)S(1)} collective-permute-done((bf16[128,768]{1,0:T(8,128)(2,1)S(1)}, bf16[128,768]{1,0:T(8,128)(2,1)S(1)}, u32[]{:S(2)}, u32[]{:S(2)}) %collective-permute-start.15) | collective-permute-done | bytes 196640 | tf_op jit(solution)/shard_map/ppermute | solution.py:291
  100.5 5.5 %collective-permute-done.25.refs_5_ = bf16[128,768]{1,0:T(8,128)(2,1)S(1)} collective-permute-done((bf16[128,768]{1,0:T(8,128)(2,1)S(1)}, bf16[128,768]{1,0:T(8,128)(2,1)S(1)}, u32[]{:S(2)}, u32[]{:S(2)}) %collective-permute-start.25) | collective-permute-done | bytes 196640 | tf_op jit(solution)/shard_map/ppermute | solution.py:291
  106.0 10.9 %collective-permute-done.26.refs_6_ = bf16[128,768]{1,0:T(8,128)(2,1)S(1)} collective-permute-done((bf16[128,768]{1,0:T(8,128)(2,1)S(1)}, bf16[128,768]{1,0:T(8,128)(2,1)S(1)}, u32[]{:S(2)}, u32[]{:S(2)}) %collective-permute-start.26) | collective-permute-done | bytes 196640 | tf_op jit(solution)/shard_map/ppermute | solution.py:291
  (89 shorter events, 23.9 us)
Async XLA Ops:
  0.9 26.1 %collective-permute-start.6 = (bf16[128,768]{1,0:T(8,128)(2,1)S(1)}, bf16[128,768]{1,0:T(8,128)(2,1)S(1)}, u32[]{:S(2)}, u32[]{:S(2)}) collective-permute-start(bf16[128,768]{1,0:T(8,128)(2,1)S(1)} %slice.6.refs_2_), channel_id=1, source_target_pairs={{0,4},{4,0},{8,12},{12,8},{16,20},{20,16},{24,28},{28,24},{1,5},{5... | collective-permute-start | bytes 589832 | tf_op jit(solution)/shard_map/ppermute | solution.py:294
  1.5 13.2 %collective-permute-start.2 = (bf16[128,768]{1,0:T(8,128)(2,1)S(1)}, bf16[128,768]{1,0:T(8,128)(2,1)S(1)}, u32[]{:S(2)}, u32[]{:S(2)}) collective-permute-start(bf16[128,768]{1,0:T(8,128)(2,1)S(1)} %slice.6.refs_2_), channel_id=1, source_target_pairs={{0,1},{1,0},{2,3},{3,2},{4,5},{5,4},{6,7},{7,6},{8,9},{9,8},{10,11... | collective-permute-start | bytes 589832 | tf_op jit(solution)/shard_map/ppermute | solution.py:291
  4.1 17.1 %collective-permute-start.1 = (bf16[128,768]{1,0:T(8,128)(2,1)S(1)}, bf16[128,768]{1,0:T(8,128)(2,1)S(1)}, u32[]{:S(2)}, u32[]{:S(2)}) collective-permute-start(bf16[128,768]{1,0:T(8,128)(2,1)S(1)} %slice.6.refs_2_), channel_id=1, source_target_pairs={{0,2},{1,3},{2,0},{3,1},{4,6},{5,7},{6,4},{7,5},{8,10},{9,11},{10,... | collective-permute-start | bytes 589832 | tf_op jit(solution)/shard_map/ppermute | solution.py:291
  6.7 14.6 %collective-permute-start = (bf16[128,768]{1,0:T(8,128)(2,1)S(1)}, bf16[128,768]{1,0:T(8,128)(2,1)S(1)}, u32[]{:S(2)}, u32[]{:S(2)}) collective-permute-start(bf16[128,768]{1,0:T(8,128)(2,1)S(1)} %slice.6.refs_2_), channel_id=1, source_target_pairs={{0,3},{1,2},{2,1},{3,0},{4,7},{5,6},{6,5},{7,4},{8,11},{9,10},{10,... | collective-permute-start | bytes 589832 | tf_op jit(solution)/shard_map/ppermute | solution.py:291
  21.3 6.9 %collective-permute-start.7 = (bf16[128,768]{1,0:T(8,128)(2,1)S(1)}, bf16[128,768]{1,0:T(8,128)(2,1)S(1)}, u32[]{:S(2)}, u32[]{:S(2)}) collective-permute-start(bf16[128,768]{1,0:T(8,128)(2,1)S(1)} %collective-permute-done.refs_3_), channel_id=1, source_target_pairs={{0,4},{4,0},{8,12},{12,8},{16,20},{20,16},{24,28},{28,24},{1,5},{5... | collective-permute-start | bytes 589832 | tf_op jit(solution)/shard_map/ppermute | solution.py:294
  22.4 7.2 %collective-permute-start.8 = (bf16[128,768]{1,0:T(8,128)(2,1)S(1)}, bf16[128,768]{1,0:T(8,128)(2,1)S(1)}, u32[]{:S(2)}, u32[]{:S(2)}) collective-permute-start(bf16[128,768]{1,0:T(8,128)(2,1)S(1)} %collective-permute-done.1.refs_4_), channel_id=1, source_target_pairs={{0,4},{4,0},{8,12},{12,8},{16,20},{20,16},{24,28},{28,24},{1,5},{5... | collective-permute-start | bytes 589832 | tf_op jit(solution)/shard_map/ppermute | solution.py:294
  22.9 6.7 %collective-permute-start.9 = (bf16[128,768]{1,0:T(8,128)(2,1)S(1)}, bf16[128,768]{1,0:T(8,128)(2,1)S(1)}, u32[]{:S(2)}, u32[]{:S(2)}) collective-permute-start(bf16[128,768]{1,0:T(8,128)(2,1)S(1)} %collective-permute-done.2.refs_5_), channel_id=1, source_target_pairs={{0,4},{4,0},{8,12},{12,8},{16,20},{20,16},{24,28},{28,24},{1,5},{5... | collective-permute-start | bytes 589832 | tf_op jit(solution)/shard_map/ppermute | solution.py:294
  23.0 13.3 %collective-permute-start.5 = (bf16[128,768]{1,0:T(8,128)(2,1)S(1)}, bf16[128,768]{1,0:T(8,128)(2,1)S(1)}, u32[]{:S(2)}, u32[]{:S(2)}) collective-permute-start(bf16[128,768]{1,0:T(8,128)(2,1)S(1)} %slice.7.refs_2_), channel_id=1, source_target_pairs={{0,1},{1,0},{2,3},{3,2},{4,5},{5,4},{6,7},{7,6},{8,9},{9,8},{10,11... | collective-permute-start | bytes 589832 | tf_op jit(solution)/shard_map/ppermute | solution.py:291
  27.0 17.1 %collective-permute-start.4 = (bf16[128,768]{1,0:T(8,128)(2,1)S(1)}, bf16[128,768]{1,0:T(8,128)(2,1)S(1)}, u32[]{:S(2)}, u32[]{:S(2)}) collective-permute-start(bf16[128,768]{1,0:T(8,128)(2,1)S(1)} %slice.7.refs_2_), channel_id=1, source_target_pairs={{0,2},{1,3},{2,0},{3,1},{4,6},{5,7},{6,4},{7,5},{8,10},{9,11},{10,... | collective-permute-start | bytes 589832 | tf_op jit(solution)/shard_map/ppermute | solution.py:291
  28.1 16.0 %collective-permute-start.3 = (bf16[128,768]{1,0:T(8,128)(2,1)S(1)}, bf16[128,768]{1,0:T(8,128)(2,1)S(1)}, u32[]{:S(2)}, u32[]{:S(2)}) collective-permute-start(bf16[128,768]{1,0:T(8,128)(2,1)S(1)} %slice.7.refs_2_), channel_id=1, source_target_pairs={{0,3},{1,2},{2,1},{3,0},{4,7},{5,6},{6,5},{7,4},{8,11},{9,10},{10,... | collective-permute-start | bytes 589832 | tf_op jit(solution)/shard_map/ppermute | solution.py:291
  29.6 19.5 %collective-permute-start.17 = (bf16[128,768]{1,0:T(8,128)(2,1)S(1)}, bf16[128,768]{1,0:T(8,128)(2,1)S(1)}, u32[]{:S(2)}, u32[]{:S(2)}) collective-permute-start(bf16[128,768]{1,0:T(8,128)(2,1)S(1)} %slice.7.refs_2_), channel_id=1, source_target_pairs={{0,4},{4,0},{8,12},{12,8},{16,20},{20,16},{24,28},{28,24},{1,5},{5... | collective-permute-start | bytes 589832 | tf_op jit(solution)/shard_map/ppermute | solution.py:294
  46.0 13.0 %collective-permute-start.12 = (bf16[256,768]{1,0:T(8,128)(2,1)S(1)}, bf16[256,768]{1,0:T(8,128)(2,1)S(1)}, u32[]{:S(2)}, u32[]{:S(2)}) collective-permute-start(bf16[256,768]{1,0:T(8,128)(2,1)S(1)} %shard_map.47.refs_2_), channel_id=1, source_target_pairs={{0,24},{4,28},{8,16},{12,20},{16,8},{20,12},{24,0},{28,4},{1,25},{... | collective-permute-start | bytes 1179656 | tf_op jit(solution)/shard_map/ppermute | solution.py:294
  49.1 18.4 %collective-permute-start.11 = (bf16[256,768]{1,0:T(8,128)(2,1)S(1)}, bf16[256,768]{1,0:T(8,128)(2,1)S(1)}, u32[]{:S(2)}, u32[]{:S(2)}) collective-permute-start(bf16[256,768]{1,0:T(8,128)(2,1)S(1)} %shard_map.47.refs_2_), channel_id=1, source_target_pairs={{0,16},{4,20},{8,24},{12,28},{16,0},{20,4},{24,8},{28,12},{1,17},{... | collective-permute-start | bytes 1179656 | tf_op jit(solution)/shard_map/ppermute | solution.py:294
  49.6 17.9 %collective-permute-start.10 = (bf16[256,768]{1,0:T(8,128)(2,1)S(1)}, bf16[256,768]{1,0:T(8,128)(2,1)S(1)}, u32[]{:S(2)}, u32[]{:S(2)}) collective-permute-start(bf16[256,768]{1,0:T(8,128)(2,1)S(1)} %shard_map.47.refs_2_), channel_id=1, source_target_pairs={{0,8},{4,12},{8,0},{12,4},{16,24},{20,28},{24,16},{28,20},{1,9},{5... | collective-permute-start | bytes 1179656 | tf_op jit(solution)/shard_map/ppermute | solution.py:294
  52.1 25.1 %collective-permute-start.23 = (bf16[256,768]{1,0:T(8,128)(2,1)S(1)}, bf16[256,768]{1,0:T(8,128)(2,1)S(1)}, u32[]{:S(2)}, u32[]{:S(2)}) collective-permute-start(bf16[256,768]{1,0:T(8,128)(2,1)S(1)} %shard_map.52.refs_3_), channel_id=1, source_target_pairs={{0,24},{4,28},{8,16},{12,20},{16,8},{20,12},{24,0},{28,4},{1,25},{... | collective-permute-start | bytes 1179656 | tf_op jit(solution)/shard_map/ppermute | solution.py:294
  54.4 29.3 %collective-permute-start.22 = (bf16[256,768]{1,0:T(8,128)(2,1)S(1)}, bf16[256,768]{1,0:T(8,128)(2,1)S(1)}, u32[]{:S(2)}, u32[]{:S(2)}) collective-permute-start(bf16[256,768]{1,0:T(8,128)(2,1)S(1)} %shard_map.52.refs_3_), channel_id=1, source_target_pairs={{0,16},{4,20},{8,24},{12,28},{16,0},{20,4},{24,8},{28,12},{1,17},{... | collective-permute-start | bytes 1179656 | tf_op jit(solution)/shard_map/ppermute | solution.py:294
  59.0 24.9 %collective-permute-start.21 = (bf16[256,768]{1,0:T(8,128)(2,1)S(1)}, bf16[256,768]{1,0:T(8,128)(2,1)S(1)}, u32[]{:S(2)}, u32[]{:S(2)}) collective-permute-start(bf16[256,768]{1,0:T(8,128)(2,1)S(1)} %shard_map.52.refs_3_), channel_id=1, source_target_pairs={{0,8},{4,12},{8,0},{12,4},{16,24},{20,28},{24,16},{28,20},{1,9},{5... | collective-permute-start | bytes 1179656 | tf_op jit(solution)/shard_map/ppermute | solution.py:294
  72.8 23.3 %collective-permute-start.14 = (bf16[128,768]{1,0:T(8,128)(2,1)S(1)}, bf16[128,768]{1,0:T(8,128)(2,1)S(1)}, u32[]{:S(2)}, u32[]{:S(2)}) collective-permute-start(bf16[128,768]{1,0:T(8,128)(2,1)S(1)} %get-tuple-element.41), channel_id=1, source_target_pairs={{0,3},{1,2},{2,1},{3,0},{4,7},{5,6},{6,5},{7,4},{8,11},{9,10},{10,... | collective-permute-start | bytes 589832 | tf_op jit(solution)/shard_map/ppermute | solution.py:291
  85.2 6.4 %collective-permute-start.24 = (bf16[128,384]{1,0:T(8,128)(2,1)S(1)}, bf16[128,384]{1,0:T(8,128)(2,1)S(1)}, u32[]{:S(2)}, u32[]{:S(2)}) collective-permute-start(bf16[128,384]{1,0:T(8,128)(2,1)S(1)} %shard_map.55), channel_id=1, source_target_pairs={{0,4},{4,0},{8,12},{12,8},{16,20},{20,16},{24,28},{28,24},{1,5},{5... | collective-permute-start | bytes 294920 | tf_op jit(solution)/shard_map/ppermute | solution.py:294
  85.2 15.0 %collective-permute-start.15 = (bf16[128,768]{1,0:T(8,128)(2,1)S(1)}, bf16[128,768]{1,0:T(8,128)(2,1)S(1)}, u32[]{:S(2)}, u32[]{:S(2)}) collective-permute-start(bf16[128,768]{1,0:T(8,128)(2,1)S(1)} %get-tuple-element.42), channel_id=1, source_target_pairs={{0,2},{1,3},{2,0},{3,1},{4,6},{5,7},{6,4},{7,5},{8,10},{9,11},{10,... | collective-permute-start | bytes 589832 | tf_op jit(solution)/shard_map/ppermute | solution.py:291
  90.3 10.2 %collective-permute-start.16 = (bf16[128,768]{1,0:T(8,128)(2,1)S(1)}, bf16[128,768]{1,0:T(8,128)(2,1)S(1)}, u32[]{:S(2)}, u32[]{:S(2)}) collective-permute-start(bf16[128,768]{1,0:T(8,128)(2,1)S(1)} %get-tuple-element.43), channel_id=1, source_target_pairs={{0,1},{1,0},{2,3},{3,2},{4,5},{5,4},{6,7},{7,6},{8,9},{9,8},{10,11... | collective-permute-start | bytes 589832 | tf_op jit(solution)/shard_map/ppermute | solution.py:291
  92.6 13.4 %collective-permute-start.25 = (bf16[128,768]{1,0:T(8,128)(2,1)S(1)}, bf16[128,768]{1,0:T(8,128)(2,1)S(1)}, u32[]{:S(2)}, u32[]{:S(2)}) collective-permute-start(bf16[128,768]{1,0:T(8,128)(2,1)S(1)} %get-tuple-element.54), channel_id=1, source_target_pairs={{0,3},{1,2},{2,1},{3,0},{4,7},{5,6},{6,5},{7,4},{8,11},{9,10},{10,... | collective-permute-start | bytes 589832 | tf_op jit(solution)/shard_map/ppermute | solution.py:291
  94.2 22.7 %collective-permute-start.26 = (bf16[128,768]{1,0:T(8,128)(2,1)S(1)}, bf16[128,768]{1,0:T(8,128)(2,1)S(1)}, u32[]{:S(2)}, u32[]{:S(2)}) collective-permute-start(bf16[128,768]{1,0:T(8,128)(2,1)S(1)} %get-tuple-element.55), channel_id=1, source_target_pairs={{0,2},{1,3},{2,0},{3,1},{4,6},{5,7},{6,4},{7,5},{8,10},{9,11},{10,... | collective-permute-start | bytes 589832 | tf_op jit(solution)/shard_map/ppermute | solution.py:291
  96.1 20.8 %collective-permute-start.27 = (bf16[128,768]{1,0:T(8,128)(2,1)S(1)}, bf16[128,768]{1,0:T(8,128)(2,1)S(1)}, u32[]{:S(2)}, u32[]{:S(2)}) collective-permute-start(bf16[128,768]{1,0:T(8,128)(2,1)S(1)} %get-tuple-element.56), channel_id=1, source_target_pairs={{0,1},{1,0},{2,3},{3,2},{4,5},{5,4},{6,7},{7,6},{8,9},{9,8},{10,11... | collective-permute-start | bytes 589832 | tf_op jit(solution)/shard_map/ppermute | solution.py:291
  (13 other events, 147.9 us)

commit v2 on v1

--- a/solution.py
+++ b/solution.py
@@ -163,40 +163,55 @@
         return perm_ref[device * local_slots + part * (local_slots // 2)] // frame_rows
 
     frames = [frame(me ^ m) for m in range(2 * masked)]
+
+    def weights_of(h, r):
+        q = q_ref[pl.ds(r * rows, rows), pl.ds(h * HD, HD)]
+        found = []
+        for i in range(free + masked):
+            scores = lax.dot_general(
+                q,
+                kv[i][:, pl.ds(h * HD, HD)],
+                (((1,), (1,)), ((), ())),
+                preferred_element_type=jnp.float32,
+            )
+            if i >= free:
+                half = scores.shape[1] // 2
+                at = 2 * (i - free)
+                bias = [
+                    jnp.where(frames[at + s] <= frames[r], jnp.float32(0), jnp.float32(MASKED))
+                    for s in range(2)
+                ]
+                scores = jnp.concatenate(
+                    [scores[:, :half] + bias[0], scores[:, half:] + bias[1]], axis=1
+                )
+            found.append(jnp.exp2(scores).astype(jnp.bfloat16))
+        return found
+
+    def finish_head(h, r, weights):
+        wide_cols = pl.ds(2 * h * HD, 2 * HD)
+        window = pl.ds(r * rows, rows)
+        target = window if len(sides) == 2 else slice(None)
+        acc = None
+        for i in range(free + masked):
+            values = kv[i][:, pl.ds(width + h * HD, HD)]
+            wide = jnp.concatenate([values, jnp.ones_like(values)], axis=1)
+            dot = jnp.dot(weights[i], wide, preferred_element_type=jnp.float32)
+            acc = dot if acc is None else acc + dot
+        if carried:
+            acc = acc + state_ref[window, wide_cols]
+        if final:
+            out_ref[target, pl.ds(h * HD, HD)] = (acc[:, :HD] / acc[:, HD:]).astype(jnp.bfloat16)
+        else:
+            out_ref[target, wide_cols] = acc
+
+    pending = None
     for h in range(heads):
-        cols = pl.ds(h * HD, HD)
-        wide_cols = pl.ds(2 * h * HD, 2 * HD)
         for r in sides:
-            window = pl.ds(r * rows, rows)
-            target = window if len(sides) == 2 else slice(None)
-            q = q_ref[window, cols]
-            if carried:
-                acc = state_ref[window, wide_cols]
-            else:
-                acc = jnp.zeros((rows, 2 * HD), jnp.float32)
-            for i in range(free + masked):
-                keys = kv[i][:, cols]
-                values = kv[i][:, pl.ds(width + h * HD, HD)]
-                scores = lax.dot_general(
-                    q, keys, (((1,), (1,)), ((), ())), preferred_element_type=jnp.float32
-                )
-                if i >= free:
-                    half = scores.shape[1] // 2
-                    at = 2 * (i - free)
-                    bias = [
-                        jnp.where(frames[at + s] <= frames[r], jnp.float32(0), jnp.float32(MASKED))
-                        for s in range(2)
-                    ]
-                    scores = jnp.concatenate(
-                        [scores[:, :half] + bias[0], scores[:, half:] + bias[1]], axis=1
-                    )
-                weights = jnp.exp2(scores).astype(jnp.bfloat16)
-                wide = jnp.concatenate([values, jnp.ones_like(values)], axis=1)
-                acc += jnp.dot(weights, wide, preferred_element_type=jnp.float32)
-            if final:
-                out_ref[target, cols] = (acc[:, :HD] / acc[:, HD:]).astype(jnp.bfloat16)
-            else:
-                out_ref[target, wide_cols] = acc
+            weights = weights_of(h, r)
+            if pending is not None:
+                finish_head(*pending)
+            pending = (h, r, weights)
+    finish_head(*pending)
 
 
 def attend(block_perm, q, state, free, masked, part, local_slots, sides, final):

time: 118 us -> 118 us (level)
  transfers between devices with their start and end apart: 28 -> 28, of which waited for: 12 -> 12; matrix products, arithmetic and copies ran while one was open for 3% -> 3% of each run, Pallas kernels for 16% -> 15%
where the time goes in v2:
time: 118 us
  waiting for transfers between devices  55 us (47%)
  starting transfers between devices  33.5 us (28%)
  Pallas kernels  19.2 us (16%)
  local copies, waits for them, and re-layouts  7.71 us (7%)
  other arithmetic  2.05 us (2%)
    ppermute x12, waiting for transfers between devices, over_levels(): return lax.ppermute(x, 'head', [(i, i ^ k) for i in range(levels)])  36.6 us
    ppermute x12, starting transfers between devices, over_levels(): return lax.ppermute(x, 'head', [(i, i ^ k) for i in range(levels)])  23.8 us
    ppermute x16, waiting for transfers between devices, over_ctx(): return lax.ppermute(x, 'ctx', [(i, i ^ mask) for i in range(ctx)])  18.4 us
    pallas_call x12, Pallas kernels, vmem_call(): pl.pallas_call(kernel, in_specs=[pl.BlockSpec(memory_space=pltpu.SMEM)] *...  16 us
    ppermute x16, starting transfers between devices, over_ctx(): return lax.ppermute(x, 'ctx', [(i, i ^ mask) for i in range(ctx)])  9.77 us
    unnamed x18, local copies, waits for them, and re-layouts  5.88 us
    pallas_call x1, Pallas kernels, fetch(): pl.pallas_call(fetch_kernel, in_specs=[pl.BlockSpec(memory_space=pltpu.Me...  3.16 us
  transfers between devices with their start and end apart: 28, of which 12 were waited for; matrix products, arithmetic and copies ran while one was open for 3% of the time, Pallas kernels for 15%

profile of v2, /device:TPU:0, one launch (start us, length us, event | category | flops | bytes accessed | tf_op | source)
XLA Modules:
  0.0 117.8 jit_solution(9286361040563100490)
XLA Ops:
  1.5 2.6 %collective-permute-start.2 = (bf16[128,768]{1,0:T(8,128)(2,1)S(1)}, bf16[128,768]{1,0:T(8,128)(2,1)S(1)}, u32[]{:S(2)}, u32[]{:S(2)}) collective-permute-start(bf16[128,768]{1,0:T(8,128)(2,1)S(1)} %slice.6.refs_2_), channel_id=1, source_target_pairs={{0,1},{1,0},{2,3},{3,2},{4,5},{5,4},{6,7},{7,6},{8,9},{9,8},{10,11... | collective-permute-start | bytes 589832 | tf_op jit(solution)/shard_map/ppermute | solution.py:306
  4.1 2.6 %collective-permute-start.1 = (bf16[128,768]{1,0:T(8,128)(2,1)S(1)}, bf16[128,768]{1,0:T(8,128)(2,1)S(1)}, u32[]{:S(2)}, u32[]{:S(2)}) collective-permute-start(bf16[128,768]{1,0:T(8,128)(2,1)S(1)} %slice.6.refs_2_), channel_id=1, source_target_pairs={{0,2},{1,3},{2,0},{3,1},{4,6},{5,7},{6,4},{7,5},{8,10},{9,11},{10,... | collective-permute-start | bytes 589832 | tf_op jit(solution)/shard_map/ppermute | solution.py:306
  8.5 3.2 %fetch.1.refs_10_ = bf16[3,3072,384]{2,1,0:T(8,128)(2,1)S(1)} custom-call(bf16[3,3072,768]{2,1,0:T(8,128)(2,1)} %w_ref.1), custom_call_target="tpu_custom_call" | custom-call | tf_op jit(solution)/shard_map/fetch/pallas_call | solution.py:99
  11.7 2.8 %copy-done = bf16[3,3072,384]{2,1,0:T(8,128)(2,1)} copy-done((bf16[3,3072,384]{2,1,0:T(8,128)(2,1)}, bf16[3,3072,384]{2,1,0:T(8,128)(2,1)S(1)}, u32[]{:S(2)}) %copy-start) | copy-done | bytes 7077912
  14.7 6.6 %collective-permute-done.1.refs_4_ = bf16[128,768]{1,0:T(8,128)(2,1)S(1)} collective-permute-done((bf16[128,768]{1,0:T(8,128)(2,1)S(1)}, bf16[128,768]{1,0:T(8,128)(2,1)S(1)}, u32[]{:S(2)}, u32[]{:S(2)}) %collective-permute-start.1) | collective-permute-done | bytes 196640 | tf_op jit(solution)/shard_map/ppermute | solution.py:306
  23.0 4.0 %collective-permute-start.5 = (bf16[128,768]{1,0:T(8,128)(2,1)S(1)}, bf16[128,768]{1,0:T(8,128)(2,1)S(1)}, u32[]{:S(2)}, u32[]{:S(2)}) collective-permute-start(bf16[128,768]{1,0:T(8,128)(2,1)S(1)} %slice.7.refs_2_), channel_id=1, source_target_pairs={{0,1},{1,0},{2,3},{3,2},{4,5},{5,4},{6,7},{7,6},{8,9},{9,8},{10,11... | collective-permute-start | bytes 589832 | tf_op jit(solution)/shard_map/ppermute | solution.py:306
  29.6 3.0 %copy-done.1 = bf16[3,3072,384]{2,1,0:T(8,128)(2,1)S(1)} copy-done((bf16[3,3072,384]{2,1,0:T(8,128)(2,1)S(1)}, bf16[3,3072,384]{2,1,0:T(8,128)(2,1)}, u32[]{:S(2)}) %copy-start.1) | copy-done | bytes 7077912
  34.1 2.2 %collective-permute-done.5.refs_5_ = bf16[128,768]{1,0:T(8,128)(2,1)S(1)} collective-permute-done((bf16[128,768]{1,0:T(8,128)(2,1)S(1)}, bf16[128,768]{1,0:T(8,128)(2,1)S(1)}, u32[]{:S(2)}, u32[]{:S(2)}) %collective-permute-start.5) | collective-permute-done | bytes 196640 | tf_op jit(solution)/shard_map/ppermute | solution.py:306
  36.3 7.9 %collective-permute-done.4.refs_4_ = bf16[128,768]{1,0:T(8,128)(2,1)S(1)} collective-permute-done((bf16[128,768]{1,0:T(8,128)(2,1)S(1)}, bf16[128,768]{1,0:T(8,128)(2,1)S(1)}, u32[]{:S(2)}, u32[]{:S(2)}) %collective-permute-start.4) | collective-permute-done | bytes 196640 | tf_op jit(solution)/shard_map/ppermute | solution.py:306
  44.2 1.8 %shard_map.47.refs_2_ = bf16[256,768]{1,0:T(8,128)(2,1)S(1)} custom-call(f32[256,128]{1,0:T(8,128)S(1)} %get-tuple-element.33.refs_0_, f32[256,128]{1,0:T(8,128)S(1)} %get-tuple-element.34.refs_1_, bf16[128,768]{1,0:T(8,128)(2,1)S(1)} %slice.6.refs_2_, bf16[128,768]{1,0:T(8,128)(2,1)S(1)} %collective-permute-done.refs_3_, ...), custom_call_target="tpu_custom_call" | custom-call | flops 1207959552 | tf_op jit(solution)/shard_map/pallas_call | solution.py:70
  46.0 2.5 %collective-permute-start.12 = (bf16[256,768]{1,0:T(8,128)(2,1)S(1)}, bf16[256,768]{1,0:T(8,128)(2,1)S(1)}, u32[]{:S(2)}, u32[]{:S(2)}) collective-permute-start(bf16[256,768]{1,0:T(8,128)(2,1)S(1)} %shard_map.47.refs_2_), channel_id=1, source_target_pairs={{0,24},{4,28},{8,16},{12,20},{16,8},{20,12},{24,0},{28,4},{1,25},{... | collective-permute-start | bytes 1179656 | tf_op jit(solution)/shard_map/ppermute | solution.py:309
  50.3 1.8 %shard_map.52.refs_3_ = bf16[256,768]{1,0:T(8,128)(2,1)S(1)} custom-call(f32[256,128]{1,0:T(8,128)S(1)} %get-tuple-element.44.refs_0_, f32[256,128]{1,0:T(8,128)S(1)} %get-tuple-element.45.refs_1_, bf16[128,768]{1,0:T(8,128)(2,1)S(1)} %slice.7.refs_2_, bf16[128,768]{1,0:T(8,128)(2,1)S(1)} %collective-permute-done.3.refs_3_, ...), custom_call_target="tpu_custom_call" | custom-call | flops 1207959552 | tf_op jit(solution)/shard_map/pallas_call | solution.py:70
  52.1 2.4 %collective-permute-start.23 = (bf16[256,768]{1,0:T(8,128)(2,1)S(1)}, bf16[256,768]{1,0:T(8,128)(2,1)S(1)}, u32[]{:S(2)}, u32[]{:S(2)}) collective-permute-start(bf16[256,768]{1,0:T(8,128)(2,1)S(1)} %shard_map.52.refs_3_), channel_id=1, source_target_pairs={{0,24},{4,28},{8,16},{12,20},{16,8},{20,12},{24,0},{28,4},{1,25},{... | collective-permute-start | bytes 1179656 | tf_op jit(solution)/shard_map/ppermute | solution.py:309
  54.9 4.1 %collective-permute-done.12.refs_5_ = bf16[256,768]{1,0:T(8,128)(2,1)S(1)} collective-permute-done((bf16[256,768]{1,0:T(8,128)(2,1)S(1)}, bf16[256,768]{1,0:T(8,128)(2,1)S(1)}, u32[]{:S(2)}, u32[]{:S(2)}) %collective-permute-start.12) | collective-permute-done | bytes 393248 | tf_op jit(solution)/shard_map/ppermute | solution.py:309
  60.5 7.0 %collective-permute-done.11.refs_4_ = bf16[256,768]{1,0:T(8,128)(2,1)S(1)} collective-permute-done((bf16[256,768]{1,0:T(8,128)(2,1)S(1)}, bf16[256,768]{1,0:T(8,128)(2,1)S(1)}, u32[]{:S(2)}, u32[]{:S(2)}) %collective-permute-start.11) | collective-permute-done | bytes 393248 | tf_op jit(solution)/shard_map/ppermute | solution.py:309
  72.5 2.5 %collective-permute-start.14 = (bf16[128,768]{1,0:T(8,128)(2,1)S(1)}, bf16[128,768]{1,0:T(8,128)(2,1)S(1)}, u32[]{:S(2)}, u32[]{:S(2)}) collective-permute-start(bf16[128,768]{1,0:T(8,128)(2,1)S(1)} %get-tuple-element.41), channel_id=1, source_target_pairs={{0,3},{1,2},{2,1},{3,0},{4,7},{5,6},{6,5},{7,4},{8,11},{9,10},{10,... | collective-permute-start | bytes 589832 | tf_op jit(solution)/shard_map/ppermute | solution.py:306
  75.0 1.8 %shard_map.53.refs_2_ = f32[256,768]{1,0:T(8,128)S(1)} custom-call(s32[32]{0:T(128)S(1)} %copy-done.2, bf16[256,384]{1,0:T(8,128)(2,1)S(1)} %shard_map.51.refs_1_, bf16[256,768]{1,0:T(8,128)(2,1)S(1)} %shard_map.47.refs_2_, bf16[256,768]{1,0:T(8,128)(2,1)S(1)} %collective-permute-done.10.refs_3_, bf16[256,768]{1,0:T(8,128)(2,1)S(1)} %collective-permute-done.11.refs_4_, ...), custom_call_target="tpu_custom_call" | custom-call | flops 805306368 | tf_op jit(solution)/shard_map/pallas_call | solution.py:70
  76.8 7.0 %collective-permute-done.22.refs_5_ = bf16[256,768]{1,0:T(8,128)(2,1)S(1)} collective-permute-done((bf16[256,768]{1,0:T(8,128)(2,1)S(1)}, bf16[256,768]{1,0:T(8,128)(2,1)S(1)}, u32[]{:S(2)}, u32[]{:S(2)}) %collective-permute-start.22) | collective-permute-done | bytes 393248 | tf_op jit(solution)/shard_map/ppermute | solution.py:309
  85.2 5.0 %collective-permute-start.15 = (bf16[128,768]{1,0:T(8,128)(2,1)S(1)}, bf16[128,768]{1,0:T(8,128)(2,1)S(1)}, u32[]{:S(2)}, u32[]{:S(2)}) collective-permute-start(bf16[128,768]{1,0:T(8,128)(2,1)S(1)} %get-tuple-element.42), channel_id=1, source_target_pairs={{0,2},{1,3},{2,0},{3,1},{4,6},{5,7},{6,4},{7,5},{8,10},{9,11},{10,... | collective-permute-start | bytes 589832 | tf_op jit(solution)/shard_map/ppermute | solution.py:306
  92.4 1.6 %collective-permute-start.25 = (bf16[128,768]{1,0:T(8,128)(2,1)S(1)}, bf16[128,768]{1,0:T(8,128)(2,1)S(1)}, u32[]{:S(2)}, u32[]{:S(2)}) collective-permute-start(bf16[128,768]{1,0:T(8,128)(2,1)S(1)} %get-tuple-element.54), channel_id=1, source_target_pairs={{0,3},{1,2},{2,1},{3,0},{4,7},{5,6},{6,5},{7,4},{8,11},{9,10},{10,... | collective-permute-start | bytes 589832 | tf_op jit(solution)/shard_map/ppermute | solution.py:306
  94.0 2.0 %collective-permute-start.26 = (bf16[128,768]{1,0:T(8,128)(2,1)S(1)}, bf16[128,768]{1,0:T(8,128)(2,1)S(1)}, u32[]{:S(2)}, u32[]{:S(2)}) collective-permute-start(bf16[128,768]{1,0:T(8,128)(2,1)S(1)} %get-tuple-element.55), channel_id=1, source_target_pairs={{0,2},{1,3},{2,0},{3,1},{4,6},{5,7},{6,4},{7,5},{8,10},{9,11},{10,... | collective-permute-start | bytes 589832 | tf_op jit(solution)/shard_map/ppermute | solution.py:306
  96.9 3.3 %collective-permute-done.15.refs_2_ = bf16[128,768]{1,0:T(8,128)(2,1)S(1)} collective-permute-done((bf16[128,768]{1,0:T(8,128)(2,1)S(1)}, bf16[128,768]{1,0:T(8,128)(2,1)S(1)}, u32[]{:S(2)}, u32[]{:S(2)}) %collective-permute-start.15) | collective-permute-done | bytes 196640 | tf_op jit(solution)/shard_map/ppermute | solution.py:306
  100.4 5.5 %collective-permute-done.25.refs_5_ = bf16[128,768]{1,0:T(8,128)(2,1)S(1)} collective-permute-done((bf16[128,768]{1,0:T(8,128)(2,1)S(1)}, bf16[128,768]{1,0:T(8,128)(2,1)S(1)}, u32[]{:S(2)}, u32[]{:S(2)}) %collective-permute-start.25) | collective-permute-done | bytes 196640 | tf_op jit(solution)/shard_map/ppermute | solution.py:306
  105.9 10.9 %collective-permute-done.26.refs_6_ = bf16[128,768]{1,0:T(8,128)(2,1)S(1)} collective-permute-done((bf16[128,768]{1,0:T(8,128)(2,1)S(1)}, bf16[128,768]{1,0:T(8,128)(2,1)S(1)}, u32[]{:S(2)}, u32[]{:S(2)}) %collective-permute-start.26) | collective-permute-done | bytes 196640 | tf_op jit(solution)/shard_map/ppermute | solution.py:306
  (89 shorter events, 23.5 us)
Async XLA Ops:
  0.9 26.1 %collective-permute-start.6 = (bf16[128,768]{1,0:T(8,128)(2,1)S(1)}, bf16[128,768]{1,0:T(8,128)(2,1)S(1)}, u32[]{:S(2)}, u32[]{:S(2)}) collective-permute-start(bf16[128,768]{1,0:T(8,128)(2,1)S(1)} %slice.6.refs_2_), channel_id=1, source_target_pairs={{0,4},{4,0},{8,12},{12,8},{16,20},{20,16},{24,28},{28,24},{1,5},{5... | collective-permute-start | bytes 589832 | tf_op jit(solution)/shard_map/ppermute | solution.py:309
  1.5 13.2 %collective-permute-start.2 = (bf16[128,768]{1,0:T(8,128)(2,1)S(1)}, bf16[128,768]{1,0:T(8,128)(2,1)S(1)}, u32[]{:S(2)}, u32[]{:S(2)}) collective-permute-start(bf16[128,768]{1,0:T(8,128)(2,1)S(1)} %slice.6.refs_2_), channel_id=1, source_target_pairs={{0,1},{1,0},{2,3},{3,2},{4,5},{5,4},{6,7},{7,6},{8,9},{9,8},{10,11... | collective-permute-start | bytes 589832 | tf_op jit(solution)/shard_map/ppermute | solution.py:306
  4.1 17.1 %collective-permute-start.1 = (bf16[128,768]{1,0:T(8,128)(2,1)S(1)}, bf16[128,768]{1,0:T(8,128)(2,1)S(1)}, u32[]{:S(2)}, u32[]{:S(2)}) collective-permute-start(bf16[128,768]{1,0:T(8,128)(2,1)S(1)} %slice.6.refs_2_), channel_id=1, source_target_pairs={{0,2},{1,3},{2,0},{3,1},{4,6},{5,7},{6,4},{7,5},{8,10},{9,11},{10,... | collective-permute-start | bytes 589832 | tf_op jit(solution)/shard_map/ppermute | solution.py:306
  6.7 14.6 %collective-permute-start = (bf16[128,768]{1,0:T(8,128)(2,1)S(1)}, bf16[128,768]{1,0:T(8,128)(2,1)S(1)}, u32[]{:S(2)}, u32[]{:S(2)}) collective-permute-start(bf16[128,768]{1,0:T(8,128)(2,1)S(1)} %slice.6.refs_2_), channel_id=1, source_target_pairs={{0,3},{1,2},{2,1},{3,0},{4,7},{5,6},{6,5},{7,4},{8,11},{9,10},{10,... | collective-permute-start | bytes 589832 | tf_op jit(solution)/shard_map/ppermute | solution.py:306
  21.3 6.9 %collective-permute-start.7 = (bf16[128,768]{1,0:T(8,128)(2,1)S(1)}, bf16[128,768]{1,0:T(8,128)(2,1)S(1)}, u32[]{:S(2)}, u32[]{:S(2)}) collective-permute-start(bf16[128,768]{1,0:T(8,128)(2,1)S(1)} %collective-permute-done.refs_3_), channel_id=1, source_target_pairs={{0,4},{4,0},{8,12},{12,8},{16,20},{20,16},{24,28},{28,24},{1,5},{5... | collective-permute-start | bytes 589832 | tf_op jit(solution)/shard_map/ppermute | solution.py:309
  22.4 7.2 %collective-permute-start.8 = (bf16[128,768]{1,0:T(8,128)(2,1)S(1)}, bf16[128,768]{1,0:T(8,128)(2,1)S(1)}, u32[]{:S(2)}, u32[]{:S(2)}) collective-permute-start(bf16[128,768]{1,0:T(8,128)(2,1)S(1)} %collective-permute-done.1.refs_4_), channel_id=1, source_target_pairs={{0,4},{4,0},{8,12},{12,8},{16,20},{20,16},{24,28},{28,24},{1,5},{5... | collective-permute-start | bytes 589832 | tf_op jit(solution)/shard_map/ppermute | solution.py:309
  22.9 6.7 %collective-permute-start.9 = (bf16[128,768]{1,0:T(8,128)(2,1)S(1)}, bf16[128,768]{1,0:T(8,128)(2,1)S(1)}, u32[]{:S(2)}, u32[]{:S(2)}) collective-permute-start(bf16[128,768]{1,0:T(8,128)(2,1)S(1)} %collective-permute-done.2.refs_5_), channel_id=1, source_target_pairs={{0,4},{4,0},{8,12},{12,8},{16,20},{20,16},{24,28},{28,24},{1,5},{5... | collective-permute-start | bytes 589832 | tf_op jit(solution)/shard_map/ppermute | solution.py:309
  23.0 13.3 %collective-permute-start.5 = (bf16[128,768]{1,0:T(8,128)(2,1)S(1)}, bf16[128,768]{1,0:T(8,128)(2,1)S(1)}, u32[]{:S(2)}, u32[]{:S(2)}) collective-permute-start(bf16[128,768]{1,0:T(8,128)(2,1)S(1)} %slice.7.refs_2_), channel_id=1, source_target_pairs={{0,1},{1,0},{2,3},{3,2},{4,5},{5,4},{6,7},{7,6},{8,9},{9,8},{10,11... | collective-permute-start | bytes 589832 | tf_op jit(solution)/shard_map/ppermute | solution.py:306
  27.0 17.1 %collective-permute-start.4 = (bf16[128,768]{1,0:T(8,128)(2,1)S(1)}, bf16[128,768]{1,0:T(8,128)(2,1)S(1)}, u32[]{:S(2)}, u32[]{:S(2)}) collective-permute-start(bf16[128,768]{1,0:T(8,128)(2,1)S(1)} %slice.7.refs_2_), channel_id=1, source_target_pairs={{0,2},{1,3},{2,0},{3,1},{4,6},{5,7},{6,4},{7,5},{8,10},{9,11},{10,... | collective-permute-start | bytes 589832 | tf_op jit(solution)/shard_map/ppermute | solution.py:306
  28.1 16.0 %collective-permute-start.3 = (bf16[128,768]{1,0:T(8,128)(2,1)S(1)}, bf16[128,768]{1,0:T(8,128)(2,1)S(1)}, u32[]{:S(2)}, u32[]{:S(2)}) collective-permute-start(bf16[128,768]{1,0:T(8,128)(2,1)S(1)} %slice.7.refs_2_), channel_id=1, source_target_pairs={{0,3},{1,2},{2,1},{3,0},{4,7},{5,6},{6,5},{7,4},{8,11},{9,10},{10,... | collective-permute-start | bytes 589832 | tf_op jit(solution)/shard_map/ppermute | solution.py:306
  29.6 19.5 %collective-permute-start.17 = (bf16[128,768]{1,0:T(8,128)(2,1)S(1)}, bf16[128,768]{1,0:T(8,128)(2,1)S(1)}, u32[]{:S(2)}, u32[]{:S(2)}) collective-permute-start(bf16[128,768]{1,0:T(8,128)(2,1)S(1)} %slice.7.refs_2_), channel_id=1, source_target_pairs={{0,4},{4,0},{8,12},{12,8},{16,20},{20,16},{24,28},{28,24},{1,5},{5... | collective-permute-start | bytes 589832 | tf_op jit(solution)/shard_map/ppermute | solution.py:309
  46.0 13.0 %collective-permute-start.12 = (bf16[256,768]{1,0:T(8,128)(2,1)S(1)}, bf16[256,768]{1,0:T(8,128)(2,1)S(1)}, u32[]{:S(2)}, u32[]{:S(2)}) collective-permute-start(bf16[256,768]{1,0:T(8,128)(2,1)S(1)} %shard_map.47.refs_2_), channel_id=1, source_target_pairs={{0,24},{4,28},{8,16},{12,20},{16,8},{20,12},{24,0},{28,4},{1,25},{... | collective-permute-start | bytes 1179656 | tf_op jit(solution)/shard_map/ppermute | solution.py:309
  49.1 18.4 %collective-permute-start.11 = (bf16[256,768]{1,0:T(8,128)(2,1)S(1)}, bf16[256,768]{1,0:T(8,128)(2,1)S(1)}, u32[]{:S(2)}, u32[]{:S(2)}) collective-permute-start(bf16[256,768]{1,0:T(8,128)(2,1)S(1)} %shard_map.47.refs_2_), channel_id=1, source_target_pairs={{0,16},{4,20},{8,24},{12,28},{16,0},{20,4},{24,8},{28,12},{1,17},{... | collective-permute-start | bytes 1179656 | tf_op jit(solution)/shard_map/ppermute | solution.py:309
  49.6 17.9 %collective-permute-start.10 = (bf16[256,768]{1,0:T(8,128)(2,1)S(1)}, bf16[256,768]{1,0:T(8,128)(2,1)S(1)}, u32[]{:S(2)}, u32[]{:S(2)}) collective-permute-start(bf16[256,768]{1,0:T(8,128)(2,1)S(1)} %shard_map.47.refs_2_), channel_id=1, source_target_pairs={{0,8},{4,12},{8,0},{12,4},{16,24},{20,28},{24,16},{28,20},{1,9},{5... | collective-permute-start | bytes 1179656 | tf_op jit(solution)/shard_map/ppermute | solution.py:309
  52.1 24.7 %collective-permute-start.23 = (bf16[256,768]{1,0:T(8,128)(2,1)S(1)}, bf16[256,768]{1,0:T(8,128)(2,1)S(1)}, u32[]{:S(2)}, u32[]{:S(2)}) collective-permute-start(bf16[256,768]{1,0:T(8,128)(2,1)S(1)} %shard_map.52.refs_3_), channel_id=1, source_target_pairs={{0,24},{4,28},{8,16},{12,20},{16,8},{20,12},{24,0},{28,4},{1,25},{... | collective-permute-start | bytes 1179656 | tf_op jit(solution)/shard_map/ppermute | solution.py:309
  54.4 29.3 %collective-permute-start.22 = (bf16[256,768]{1,0:T(8,128)(2,1)S(1)}, bf16[256,768]{1,0:T(8,128)(2,1)S(1)}, u32[]{:S(2)}, u32[]{:S(2)}) collective-permute-start(bf16[256,768]{1,0:T(8,128)(2,1)S(1)} %shard_map.52.refs_3_), channel_id=1, source_target_pairs={{0,16},{4,20},{8,24},{12,28},{16,0},{20,4},{24,8},{28,12},{1,17},{... | collective-permute-start | bytes 1179656 | tf_op jit(solution)/shard_map/ppermute | solution.py:309
  59.0 24.9 %collective-permute-start.21 = (bf16[256,768]{1,0:T(8,128)(2,1)S(1)}, bf16[256,768]{1,0:T(8,128)(2,1)S(1)}, u32[]{:S(2)}, u32[]{:S(2)}) collective-permute-start(bf16[256,768]{1,0:T(8,128)(2,1)S(1)} %shard_map.52.refs_3_), channel_id=1, source_target_pairs={{0,8},{4,12},{8,0},{12,4},{16,24},{20,28},{24,16},{28,20},{1,9},{5... | collective-permute-start | bytes 1179656 | tf_op jit(solution)/shard_map/ppermute | solution.py:309
  72.5 23.4 %collective-permute-start.14 = (bf16[128,768]{1,0:T(8,128)(2,1)S(1)}, bf16[128,768]{1,0:T(8,128)(2,1)S(1)}, u32[]{:S(2)}, u32[]{:S(2)}) collective-permute-start(bf16[128,768]{1,0:T(8,128)(2,1)S(1)} %get-tuple-element.41), channel_id=1, source_target_pairs={{0,3},{1,2},{2,1},{3,0},{4,7},{5,6},{6,5},{7,4},{8,11},{9,10},{10,... | collective-permute-start | bytes 589832 | tf_op jit(solution)/shard_map/ppermute | solution.py:306
  85.1 6.3 %collective-permute-start.24 = (bf16[128,384]{1,0:T(8,128)(2,1)S(1)}, bf16[128,384]{1,0:T(8,128)(2,1)S(1)}, u32[]{:S(2)}, u32[]{:S(2)}) collective-permute-start(bf16[128,384]{1,0:T(8,128)(2,1)S(1)} %shard_map.55), channel_id=1, source_target_pairs={{0,4},{4,0},{8,12},{12,8},{16,20},{20,16},{24,28},{28,24},{1,5},{5... | collective-permute-start | bytes 294920 | tf_op jit(solution)/shard_map/ppermute | solution.py:309
  85.2 15.0 %collective-permute-start.15 = (bf16[128,768]{1,0:T(8,128)(2,1)S(1)}, bf16[128,768]{1,0:T(8,128)(2,1)S(1)}, u32[]{:S(2)}, u32[]{:S(2)}) collective-permute-start(bf16[128,768]{1,0:T(8,128)(2,1)S(1)} %get-tuple-element.42), channel_id=1, source_target_pairs={{0,2},{1,3},{2,0},{3,1},{4,6},{5,7},{6,4},{7,5},{8,10},{9,11},{10,... | collective-permute-start | bytes 589832 | tf_op jit(solution)/shard_map/ppermute | solution.py:306
  90.2 10.2 %collective-permute-start.16 = (bf16[128,768]{1,0:T(8,128)(2,1)S(1)}, bf16[128,768]{1,0:T(8,128)(2,1)S(1)}, u32[]{:S(2)}, u32[]{:S(2)}) collective-permute-start(bf16[128,768]{1,0:T(8,128)(2,1)S(1)} %get-tuple-element.43), channel_id=1, source_target_pairs={{0,1},{1,0},{2,3},{3,2},{4,5},{5,4},{6,7},{7,6},{8,9},{9,8},{10,11... | collective-permute-start | bytes 589832 | tf_op jit(solution)/shard_map/ppermute | solution.py:306
  92.4 13.5 %collective-permute-start.25 = (bf16[128,768]{1,0:T(8,128)(2,1)S(1)}, bf16[128,768]{1,0:T(8,128)(2,1)S(1)}, u32[]{:S(2)}, u32[]{:S(2)}) collective-permute-start(bf16[128,768]{1,0:T(8,128)(2,1)S(1)} %get-tuple-element.54), channel_id=1, source_target_pairs={{0,3},{1,2},{2,1},{3,0},{4,7},{5,6},{6,5},{7,4},{8,11},{9,10},{10,... | collective-permute-start | bytes 589832 | tf_op jit(solution)/shard_map/ppermute | solution.py:306
  94.0 22.8 %collective-permute-start.26 = (bf16[128,768]{1,0:T(8,128)(2,1)S(1)}, bf16[128,768]{1,0:T(8,128)(2,1)S(1)}, u32[]{:S(2)}, u32[]{:S(2)}) collective-permute-start(bf16[128,768]{1,0:T(8,128)(2,1)S(1)} %get-tuple-element.55), channel_id=1, source_target_pairs={{0,2},{1,3},{2,0},{3,1},{4,6},{5,7},{6,4},{7,5},{8,10},{9,11},{10,... | collective-permute-start | bytes 589832 | tf_op jit(solution)/shard_map/ppermute | solution.py:306
  96.0 20.8 %collective-permute-start.27 = (bf16[128,768]{1,0:T(8,128)(2,1)S(1)}, bf16[128,768]{1,0:T(8,128)(2,1)S(1)}, u32[]{:S(2)}, u32[]{:S(2)}) collective-permute-start(bf16[128,768]{1,0:T(8,128)(2,1)S(1)} %get-tuple-element.56), channel_id=1, source_target_pairs={{0,1},{1,0},{2,3},{3,2},{4,5},{5,4},{6,7},{7,6},{8,9},{9,8},{10,11... | collective-permute-start | bytes 589832 | tf_op jit(solution)/shard_map/ppermute | solution.py:306
  (13 other events, 147.2 us)

commit v3 on v2

--- a/solution.py
+++ b/solution.py
@@ -149,7 +149,7 @@
 
 
 def attend_kernel(
-    carried, sides, final, free, masked, heads, part, local_slots, perm_ref, q_ref, *refs
+    carried, sides, final, free, masked, start, heads, part, local_slots, perm_ref, q_ref, *refs
 ):
     state_ref = refs[0] if carried else None
     kv = refs[carried : carried + free + masked]
@@ -162,7 +162,8 @@
     def frame(device):
         return perm_ref[device * local_slots + part * (local_slots // 2)] // frame_rows
 
-    frames = [frame(me ^ m) for m in range(2 * masked)]
+    asking = [frame(me ^ m) for m in range(2)]
+    frames = [frame(me ^ (2 * start + m)) for m in range(2 * masked)]
 
     def weights_of(h, r):
         q = q_ref[pl.ds(r * rows, rows), pl.ds(h * HD, HD)]
@@ -178,7 +179,7 @@
                 half = scores.shape[1] // 2
                 at = 2 * (i - free)
                 bias = [
-                    jnp.where(frames[at + s] <= frames[r], jnp.float32(0), jnp.float32(MASKED))
+                    jnp.where(frames[at + s] <= asking[r], jnp.float32(0), jnp.float32(MASKED))
                     for s in range(2)
                 ]
                 scores = jnp.concatenate(
@@ -214,7 +215,7 @@
     finish_head(*pending)
 
 
-def attend(block_perm, q, state, free, masked, part, local_slots, sides, final):
+def attend(block_perm, q, state, free, masked, start, part, local_slots, sides, final):
     rows2, width = q.shape
     heads = width // HD
     keys = sum(p.shape[0] for p in free + masked)
@@ -226,7 +227,7 @@
         out = jax.ShapeDtypeStruct((out_rows, 2 * width), jnp.float32)
     return vmem_call(
         functools.partial(
-            attend_kernel, carried, sides, final, len(free), len(masked), heads, part, local_slots
+            attend_kernel, carried, sides, final, len(free), len(masked), start, heads, part, local_slots
         ),
         [q] + ([state] if carried else []) + free + masked,
         [out],
@@ -354,11 +355,13 @@
         q, pieces = projected[part]
         state = None
         if part == 1:
-            state = attend(block_perm, q, None, projected[0][1], [], part, local_slots, (0, 1), False)
+            state = attend(block_perm, q, None, projected[0][1], pieces[:1], 0, part, local_slots, (0, 1), False)
             pieces[1:], state = lax.optimization_barrier((pieces[1:], state))
         both = []
         for side in (1, 0):
-            both.append(attend(block_perm, q, state, [], pieces, part, local_slots, (side,), True))
+            both.append(
+                attend(block_perm, q, state, [], pieces[part:], part, part, local_slots, (side,), True)
+            )
             if side == 1:
                 theirs = over_ctx(both[0], 1)
         heads_out = both[1]

time: 118 us -> 118 us (level)
  transfers between devices with their start and end apart: 28 -> 28, of which waited for: 12 -> 12; matrix products, arithmetic and copies ran while one was open for 3% -> 3% of each run, Pallas kernels for 15% -> 16%
where the time goes in v3:
time: 118 us
  waiting for transfers between devices  54.9 us (47%)
  starting transfers between devices  33.5 us (28%)
  Pallas kernels  19.2 us (16%)
  local copies, waits for them, and re-layouts  7.71 us (7%)
  other arithmetic  2.05 us (2%)
    ppermute x12, waiting for transfers between devices, over_levels(): return lax.ppermute(x, 'head', [(i, i ^ k) for i in range(levels)])  36.7 us
    ppermute x12, starting transfers between devices, over_levels(): return lax.ppermute(x, 'head', [(i, i ^ k) for i in range(levels)])  23.8 us
    ppermute x16, waiting for transfers between devices, over_ctx(): return lax.ppermute(x, 'ctx', [(i, i ^ mask) for i in range(ctx)])  18.2 us
    pallas_call x12, Pallas kernels, vmem_call(): pl.pallas_call(kernel, in_specs=[pl.BlockSpec(memory_space=pltpu.SMEM)] *...  16 us
    ppermute x16, starting transfers between devices, over_ctx(): return lax.ppermute(x, 'ctx', [(i, i ^ mask) for i in range(ctx)])  9.77 us
    unnamed x18, local copies, waits for them, and re-layouts  5.88 us
    pallas_call x1, Pallas kernels, fetch(): pl.pallas_call(fetch_kernel, in_specs=[pl.BlockSpec(memory_space=pltpu.Me...  3.16 us
  transfers between devices with their start and end apart: 28, of which 12 were waited for; matrix products, arithmetic and copies ran while one was open for 3% of the time, Pallas kernels for 16%

profile of v3, /device:TPU:0, one launch (start us, length us, event | category | flops | bytes accessed | tf_op | source)
XLA Modules:
  0.0 117.7 jit_solution(11517783024766521197)
XLA Ops:
  1.5 2.6 %collective-permute-start.2 = (bf16[128,768]{1,0:T(8,128)(2,1)S(1)}, bf16[128,768]{1,0:T(8,128)(2,1)S(1)}, u32[]{:S(2)}, u32[]{:S(2)}) collective-permute-start(bf16[128,768]{1,0:T(8,128)(2,1)S(1)} %slice.6.refs_2_), channel_id=1, source_target_pairs={{0,1},{1,0},{2,3},{3,2},{4,5},{5,4},{6,7},{7,6},{8,9},{9,8},{10,11... | collective-permute-start | bytes 589832 | tf_op jit(solution)/shard_map/ppermute | solution.py:307
  4.1 2.6 %collective-permute-start.1 = (bf16[128,768]{1,0:T(8,128)(2,1)S(1)}, bf16[128,768]{1,0:T(8,128)(2,1)S(1)}, u32[]{:S(2)}, u32[]{:S(2)}) collective-permute-start(bf16[128,768]{1,0:T(8,128)(2,1)S(1)} %slice.6.refs_2_), channel_id=1, source_target_pairs={{0,2},{1,3},{2,0},{3,1},{4,6},{5,7},{6,4},{7,5},{8,10},{9,11},{10,... | collective-permute-start | bytes 589832 | tf_op jit(solution)/shard_map/ppermute | solution.py:307
  8.5 3.2 %fetch.1.refs_10_ = bf16[3,3072,384]{2,1,0:T(8,128)(2,1)S(1)} custom-call(bf16[3,3072,768]{2,1,0:T(8,128)(2,1)} %w_ref.1), custom_call_target="tpu_custom_call" | custom-call | tf_op jit(solution)/shard_map/fetch/pallas_call | solution.py:99
  11.7 2.8 %copy-done = bf16[3,3072,384]{2,1,0:T(8,128)(2,1)} copy-done((bf16[3,3072,384]{2,1,0:T(8,128)(2,1)}, bf16[3,3072,384]{2,1,0:T(8,128)(2,1)S(1)}, u32[]{:S(2)}) %copy-start) | copy-done | bytes 7077912
  14.7 6.6 %collective-permute-done.1.refs_4_ = bf16[128,768]{1,0:T(8,128)(2,1)S(1)} collective-permute-done((bf16[128,768]{1,0:T(8,128)(2,1)S(1)}, bf16[128,768]{1,0:T(8,128)(2,1)S(1)}, u32[]{:S(2)}, u32[]{:S(2)}) %collective-permute-start.1) | collective-permute-done | bytes 196640 | tf_op jit(solution)/shard_map/ppermute | solution.py:307
  23.0 4.0 %collective-permute-start.5 = (bf16[128,768]{1,0:T(8,128)(2,1)S(1)}, bf16[128,768]{1,0:T(8,128)(2,1)S(1)}, u32[]{:S(2)}, u32[]{:S(2)}) collective-permute-start(bf16[128,768]{1,0:T(8,128)(2,1)S(1)} %slice.7.refs_2_), channel_id=1, source_target_pairs={{0,1},{1,0},{2,3},{3,2},{4,5},{5,4},{6,7},{7,6},{8,9},{9,8},{10,11... | collective-permute-start | bytes 589832 | tf_op jit(solution)/shard_map/ppermute | solution.py:307
  29.6 3.0 %copy-done.1 = bf16[3,3072,384]{2,1,0:T(8,128)(2,1)S(1)} copy-done((bf16[3,3072,384]{2,1,0:T(8,128)(2,1)S(1)}, bf16[3,3072,384]{2,1,0:T(8,128)(2,1)}, u32[]{:S(2)}) %copy-start.1) | copy-done | bytes 7077912
  34.1 2.2 %collective-permute-done.5.refs_5_ = bf16[128,768]{1,0:T(8,128)(2,1)S(1)} collective-permute-done((bf16[128,768]{1,0:T(8,128)(2,1)S(1)}, bf16[128,768]{1,0:T(8,128)(2,1)S(1)}, u32[]{:S(2)}, u32[]{:S(2)}) %collective-permute-start.5) | collective-permute-done | bytes 196640 | tf_op jit(solution)/shard_map/ppermute | solution.py:307
  36.3 7.9 %collective-permute-done.4.refs_4_ = bf16[128,768]{1,0:T(8,128)(2,1)S(1)} collective-permute-done((bf16[128,768]{1,0:T(8,128)(2,1)S(1)}, bf16[128,768]{1,0:T(8,128)(2,1)S(1)}, u32[]{:S(2)}, u32[]{:S(2)}) %collective-permute-start.4) | collective-permute-done | bytes 196640 | tf_op jit(solution)/shard_map/ppermute | solution.py:307
  44.2 1.8 %shard_map.47.refs_2_ = bf16[256,768]{1,0:T(8,128)(2,1)S(1)} custom-call(f32[256,128]{1,0:T(8,128)S(1)} %get-tuple-element.33.refs_0_, f32[256,128]{1,0:T(8,128)S(1)} %get-tuple-element.34.refs_1_, bf16[128,768]{1,0:T(8,128)(2,1)S(1)} %slice.6.refs_2_, bf16[128,768]{1,0:T(8,128)(2,1)S(1)} %collective-permute-done.refs_3_, ...), custom_call_target="tpu_custom_call" | custom-call | flops 1207959552 | tf_op jit(solution)/shard_map/pallas_call | solution.py:70
  46.0 2.5 %collective-permute-start.12 = (bf16[256,768]{1,0:T(8,128)(2,1)S(1)}, bf16[256,768]{1,0:T(8,128)(2,1)S(1)}, u32[]{:S(2)}, u32[]{:S(2)}) collective-permute-start(bf16[256,768]{1,0:T(8,128)(2,1)S(1)} %shard_map.47.refs_2_), channel_id=1, source_target_pairs={{0,24},{4,28},{8,16},{12,20},{16,8},{20,12},{24,0},{28,4},{1,25},{... | collective-permute-start | bytes 1179656 | tf_op jit(solution)/shard_map/ppermute | solution.py:310
  50.3 1.8 %shard_map.52.refs_6_ = bf16[256,768]{1,0:T(8,128)(2,1)S(1)} custom-call(f32[256,128]{1,0:T(8,128)S(1)} %get-tuple-element.44.refs_0_, f32[256,128]{1,0:T(8,128)S(1)} %get-tuple-element.45.refs_1_, bf16[128,768]{1,0:T(8,128)(2,1)S(1)} %slice.7.refs_2_, bf16[128,768]{1,0:T(8,128)(2,1)S(1)} %collective-permute-done.3.refs_3_, ...), custom_call_target="tpu_custom_call" | custom-call | flops 1207959552 | tf_op jit(solution)/shard_map/pallas_call | solution.py:70
  52.1 2.4 %collective-permute-start.23 = (bf16[256,768]{1,0:T(8,128)(2,1)S(1)}, bf16[256,768]{1,0:T(8,128)(2,1)S(1)}, u32[]{:S(2)}, u32[]{:S(2)}) collective-permute-start(bf16[256,768]{1,0:T(8,128)(2,1)S(1)} %shard_map.52.refs_6_), channel_id=1, source_target_pairs={{0,24},{4,28},{8,16},{12,20},{16,8},{20,12},{24,0},{28,4},{1,25},{... | collective-permute-start | bytes 1179656 | tf_op jit(solution)/shard_map/ppermute | solution.py:310
  54.9 4.1 %collective-permute-done.12.refs_5_ = bf16[256,768]{1,0:T(8,128)(2,1)S(1)} collective-permute-done((bf16[256,768]{1,0:T(8,128)(2,1)S(1)}, bf16[256,768]{1,0:T(8,128)(2,1)S(1)}, u32[]{:S(2)}, u32[]{:S(2)}) %collective-permute-start.12) | collective-permute-done | bytes 393248 | tf_op jit(solution)/shard_map/ppermute | solution.py:310
  60.5 7.0 %collective-permute-done.11.refs_4_ = bf16[256,768]{1,0:T(8,128)(2,1)S(1)} collective-permute-done((bf16[256,768]{1,0:T(8,128)(2,1)S(1)}, bf16[256,768]{1,0:T(8,128)(2,1)S(1)}, u32[]{:S(2)}, u32[]{:S(2)}) %collective-permute-start.11) | collective-permute-done | bytes 393248 | tf_op jit(solution)/shard_map/ppermute | solution.py:310
  72.5 2.5 %collective-permute-start.14 = (bf16[128,768]{1,0:T(8,128)(2,1)S(1)}, bf16[128,768]{1,0:T(8,128)(2,1)S(1)}, u32[]{:S(2)}, u32[]{:S(2)}) collective-permute-start(bf16[128,768]{1,0:T(8,128)(2,1)S(1)} %get-tuple-element.41), channel_id=1, source_target_pairs={{0,3},{1,2},{2,1},{3,0},{4,7},{5,6},{6,5},{7,4},{8,11},{9,10},{10,... | collective-permute-start | bytes 589832 | tf_op jit(solution)/shard_map/ppermute | solution.py:307
  75.0 1.9 %shard_map.53.refs_2_ = f32[256,768]{1,0:T(8,128)S(1)} custom-call(s32[32]{0:T(128)S(1)} %copy-done.2, bf16[256,384]{1,0:T(8,128)(2,1)S(1)} %shard_map.51.refs_1_, bf16[256,768]{1,0:T(8,128)(2,1)S(1)} %shard_map.47.refs_2_, bf16[256,768]{1,0:T(8,128)(2,1)S(1)} %collective-permute-done.10.refs_3_, bf16[256,768]{1,0:T(8,128)(2,1)S(1)} %collective-permute-done.11.refs_4_, ...), custom_call_target="tpu_custom_call" | custom-call | flops 1006632960 | tf_op jit(solution)/shard_map/pallas_call | solution.py:70
  77.0 6.8 %collective-permute-done.22.refs_4_ = bf16[256,768]{1,0:T(8,128)(2,1)S(1)} collective-permute-done((bf16[256,768]{1,0:T(8,128)(2,1)S(1)}, bf16[256,768]{1,0:T(8,128)(2,1)S(1)}, u32[]{:S(2)}, u32[]{:S(2)}) %collective-permute-start.22) | collective-permute-done | bytes 393248 | tf_op jit(solution)/shard_map/ppermute | solution.py:310
  85.1 5.0 %collective-permute-start.15 = (bf16[128,768]{1,0:T(8,128)(2,1)S(1)}, bf16[128,768]{1,0:T(8,128)(2,1)S(1)}, u32[]{:S(2)}, u32[]{:S(2)}) collective-permute-start(bf16[128,768]{1,0:T(8,128)(2,1)S(1)} %get-tuple-element.42), channel_id=1, source_target_pairs={{0,2},{1,3},{2,0},{3,1},{4,6},{5,7},{6,4},{7,5},{8,10},{9,11},{10,... | collective-permute-start | bytes 589832 | tf_op jit(solution)/shard_map/ppermute | solution.py:307
  92.3 1.6 %collective-permute-start.25 = (bf16[128,768]{1,0:T(8,128)(2,1)S(1)}, bf16[128,768]{1,0:T(8,128)(2,1)S(1)}, u32[]{:S(2)}, u32[]{:S(2)}) collective-permute-start(bf16[128,768]{1,0:T(8,128)(2,1)S(1)} %get-tuple-element.54), channel_id=1, source_target_pairs={{0,3},{1,2},{2,1},{3,0},{4,7},{5,6},{6,5},{7,4},{8,11},{9,10},{10,... | collective-permute-start | bytes 589832 | tf_op jit(solution)/shard_map/ppermute | solution.py:307
  93.9 2.0 %collective-permute-start.26 = (bf16[128,768]{1,0:T(8,128)(2,1)S(1)}, bf16[128,768]{1,0:T(8,128)(2,1)S(1)}, u32[]{:S(2)}, u32[]{:S(2)}) collective-permute-start(bf16[128,768]{1,0:T(8,128)(2,1)S(1)} %get-tuple-element.55), channel_id=1, source_target_pairs={{0,2},{1,3},{2,0},{3,1},{4,6},{5,7},{6,4},{7,5},{8,10},{9,11},{10,... | collective-permute-start | bytes 589832 | tf_op jit(solution)/shard_map/ppermute | solution.py:307
  96.8 3.4 %collective-permute-done.15.refs_2_ = bf16[128,768]{1,0:T(8,128)(2,1)S(1)} collective-permute-done((bf16[128,768]{1,0:T(8,128)(2,1)S(1)}, bf16[128,768]{1,0:T(8,128)(2,1)S(1)}, u32[]{:S(2)}, u32[]{:S(2)}) %collective-permute-start.15) | collective-permute-done | bytes 196640 | tf_op jit(solution)/shard_map/ppermute | solution.py:307
  100.3 5.5 %collective-permute-done.25.refs_5_ = bf16[128,768]{1,0:T(8,128)(2,1)S(1)} collective-permute-done((bf16[128,768]{1,0:T(8,128)(2,1)S(1)}, bf16[128,768]{1,0:T(8,128)(2,1)S(1)}, u32[]{:S(2)}, u32[]{:S(2)}) %collective-permute-start.25) | collective-permute-done | bytes 196640 | tf_op jit(solution)/shard_map/ppermute | solution.py:307
  105.8 10.9 %collective-permute-done.26.refs_6_ = bf16[128,768]{1,0:T(8,128)(2,1)S(1)} collective-permute-done((bf16[128,768]{1,0:T(8,128)(2,1)S(1)}, bf16[128,768]{1,0:T(8,128)(2,1)S(1)}, u32[]{:S(2)}, u32[]{:S(2)}) %collective-permute-start.26) | collective-permute-done | bytes 196640 | tf_op jit(solution)/shard_map/ppermute | solution.py:307
  (89 shorter events, 23.4 us)
Async XLA Ops:
  0.9 26.1 %collective-permute-start.6 = (bf16[128,768]{1,0:T(8,128)(2,1)S(1)}, bf16[128,768]{1,0:T(8,128)(2,1)S(1)}, u32[]{:S(2)}, u32[]{:S(2)}) collective-permute-start(bf16[128,768]{1,0:T(8,128)(2,1)S(1)} %slice.6.refs_2_), channel_id=1, source_target_pairs={{0,4},{4,0},{8,12},{12,8},{16,20},{20,16},{24,28},{28,24},{1,5},{5... | collective-permute-start | bytes 589832 | tf_op jit(solution)/shard_map/ppermute | solution.py:310
  1.5 13.2 %collective-permute-start.2 = (bf16[128,768]{1,0:T(8,128)(2,1)S(1)}, bf16[128,768]{1,0:T(8,128)(2,1)S(1)}, u32[]{:S(2)}, u32[]{:S(2)}) collective-permute-start(bf16[128,768]{1,0:T(8,128)(2,1)S(1)} %slice.6.refs_2_), channel_id=1, source_target_pairs={{0,1},{1,0},{2,3},{3,2},{4,5},{5,4},{6,7},{7,6},{8,9},{9,8},{10,11... | collective-permute-start | bytes 589832 | tf_op jit(solution)/shard_map/ppermute | solution.py:307
  4.1 17.1 %collective-permute-start.1 = (bf16[128,768]{1,0:T(8,128)(2,1)S(1)}, bf16[128,768]{1,0:T(8,128)(2,1)S(1)}, u32[]{:S(2)}, u32[]{:S(2)}) collective-permute-start(bf16[128,768]{1,0:T(8,128)(2,1)S(1)} %slice.6.refs_2_), channel_id=1, source_target_pairs={{0,2},{1,3},{2,0},{3,1},{4,6},{5,7},{6,4},{7,5},{8,10},{9,11},{10,... | collective-permute-start | bytes 589832 | tf_op jit(solution)/shard_map/ppermute | solution.py:307
  6.7 14.6 %collective-permute-start = (bf16[128,768]{1,0:T(8,128)(2,1)S(1)}, bf16[128,768]{1,0:T(8,128)(2,1)S(1)}, u32[]{:S(2)}, u32[]{:S(2)}) collective-permute-start(bf16[128,768]{1,0:T(8,128)(2,1)S(1)} %slice.6.refs_2_), channel_id=1, source_target_pairs={{0,3},{1,2},{2,1},{3,0},{4,7},{5,6},{6,5},{7,4},{8,11},{9,10},{10,... | collective-permute-start | bytes 589832 | tf_op jit(solution)/shard_map/ppermute | solution.py:307
  21.3 6.9 %collective-permute-start.7 = (bf16[128,768]{1,0:T(8,128)(2,1)S(1)}, bf16[128,768]{1,0:T(8,128)(2,1)S(1)}, u32[]{:S(2)}, u32[]{:S(2)}) collective-permute-start(bf16[128,768]{1,0:T(8,128)(2,1)S(1)} %collective-permute-done.refs_3_), channel_id=1, source_target_pairs={{0,4},{4,0},{8,12},{12,8},{16,20},{20,16},{24,28},{28,24},{1,5},{5... | collective-permute-start | bytes 589832 | tf_op jit(solution)/shard_map/ppermute | solution.py:310
  22.4 7.2 %collective-permute-start.8 = (bf16[128,768]{1,0:T(8,128)(2,1)S(1)}, bf16[128,768]{1,0:T(8,128)(2,1)S(1)}, u32[]{:S(2)}, u32[]{:S(2)}) collective-permute-start(bf16[128,768]{1,0:T(8,128)(2,1)S(1)} %collective-permute-done.1.refs_4_), channel_id=1, source_target_pairs={{0,4},{4,0},{8,12},{12,8},{16,20},{20,16},{24,28},{28,24},{1,5},{5... | collective-permute-start | bytes 589832 | tf_op jit(solution)/shard_map/ppermute | solution.py:310
  22.9 6.7 %collective-permute-start.9 = (bf16[128,768]{1,0:T(8,128)(2,1)S(1)}, bf16[128,768]{1,0:T(8,128)(2,1)S(1)}, u32[]{:S(2)}, u32[]{:S(2)}) collective-permute-start(bf16[128,768]{1,0:T(8,128)(2,1)S(1)} %collective-permute-done.2.refs_5_), channel_id=1, source_target_pairs={{0,4},{4,0},{8,12},{12,8},{16,20},{20,16},{24,28},{28,24},{1,5},{5... | collective-permute-start | bytes 589832 | tf_op jit(solution)/shard_map/ppermute | solution.py:310
  23.0 13.3 %collective-permute-start.5 = (bf16[128,768]{1,0:T(8,128)(2,1)S(1)}, bf16[128,768]{1,0:T(8,128)(2,1)S(1)}, u32[]{:S(2)}, u32[]{:S(2)}) collective-permute-start(bf16[128,768]{1,0:T(8,128)(2,1)S(1)} %slice.7.refs_2_), channel_id=1, source_target_pairs={{0,1},{1,0},{2,3},{3,2},{4,5},{5,4},{6,7},{7,6},{8,9},{9,8},{10,11... | collective-permute-start | bytes 589832 | tf_op jit(solution)/shard_map/ppermute | solution.py:307
  27.0 17.1 %collective-permute-start.4 = (bf16[128,768]{1,0:T(8,128)(2,1)S(1)}, bf16[128,768]{1,0:T(8,128)(2,1)S(1)}, u32[]{:S(2)}, u32[]{:S(2)}) collective-permute-start(bf16[128,768]{1,0:T(8,128)(2,1)S(1)} %slice.7.refs_2_), channel_id=1, source_target_pairs={{0,2},{1,3},{2,0},{3,1},{4,6},{5,7},{6,4},{7,5},{8,10},{9,11},{10,... | collective-permute-start | bytes 589832 | tf_op jit(solution)/shard_map/ppermute | solution.py:307
  28.1 16.0 %collective-permute-start.3 = (bf16[128,768]{1,0:T(8,128)(2,1)S(1)}, bf16[128,768]{1,0:T(8,128)(2,1)S(1)}, u32[]{:S(2)}, u32[]{:S(2)}) collective-permute-start(bf16[128,768]{1,0:T(8,128)(2,1)S(1)} %slice.7.refs_2_), channel_id=1, source_target_pairs={{0,3},{1,2},{2,1},{3,0},{4,7},{5,6},{6,5},{7,4},{8,11},{9,10},{10,... | collective-permute-start | bytes 589832 | tf_op jit(solution)/shard_map/ppermute | solution.py:307
  29.6 19.5 %collective-permute-start.17 = (bf16[128,768]{1,0:T(8,128)(2,1)S(1)}, bf16[128,768]{1,0:T(8,128)(2,1)S(1)}, u32[]{:S(2)}, u32[]{:S(2)}) collective-permute-start(bf16[128,768]{1,0:T(8,128)(2,1)S(1)} %slice.7.refs_2_), channel_id=1, source_target_pairs={{0,4},{4,0},{8,12},{12,8},{16,20},{20,16},{24,28},{28,24},{1,5},{5... | collective-permute-start | bytes 589832 | tf_op jit(solution)/shard_map/ppermute | solution.py:310
  46.0 13.0 %collective-permute-start.12 = (bf16[256,768]{1,0:T(8,128)(2,1)S(1)}, bf16[256,768]{1,0:T(8,128)(2,1)S(1)}, u32[]{:S(2)}, u32[]{:S(2)}) collective-permute-start(bf16[256,768]{1,0:T(8,128)(2,1)S(1)} %shard_map.47.refs_2_), channel_id=1, source_target_pairs={{0,24},{4,28},{8,16},{12,20},{16,8},{20,12},{24,0},{28,4},{1,25},{... | collective-permute-start | bytes 1179656 | tf_op jit(solution)/shard_map/ppermute | solution.py:310
  49.1 18.4 %collective-permute-start.11 = (bf16[256,768]{1,0:T(8,128)(2,1)S(1)}, bf16[256,768]{1,0:T(8,128)(2,1)S(1)}, u32[]{:S(2)}, u32[]{:S(2)}) collective-permute-start(bf16[256,768]{1,0:T(8,128)(2,1)S(1)} %shard_map.47.refs_2_), channel_id=1, source_target_pairs={{0,16},{4,20},{8,24},{12,28},{16,0},{20,4},{24,8},{28,12},{1,17},{... | collective-permute-start | bytes 1179656 | tf_op jit(solution)/shard_map/ppermute | solution.py:310
  49.6 17.9 %collective-permute-start.10 = (bf16[256,768]{1,0:T(8,128)(2,1)S(1)}, bf16[256,768]{1,0:T(8,128)(2,1)S(1)}, u32[]{:S(2)}, u32[]{:S(2)}) collective-permute-start(bf16[256,768]{1,0:T(8,128)(2,1)S(1)} %shard_map.47.refs_2_), channel_id=1, source_target_pairs={{0,8},{4,12},{8,0},{12,4},{16,24},{20,28},{24,16},{28,20},{1,9},{5... | collective-permute-start | bytes 1179656 | tf_op jit(solution)/shard_map/ppermute | solution.py:310
  52.1 24.9 %collective-permute-start.23 = (bf16[256,768]{1,0:T(8,128)(2,1)S(1)}, bf16[256,768]{1,0:T(8,128)(2,1)S(1)}, u32[]{:S(2)}, u32[]{:S(2)}) collective-permute-start(bf16[256,768]{1,0:T(8,128)(2,1)S(1)} %shard_map.52.refs_6_), channel_id=1, source_target_pairs={{0,24},{4,28},{8,16},{12,20},{16,8},{20,12},{24,0},{28,4},{1,25},{... | collective-permute-start | bytes 1179656 | tf_op jit(solution)/shard_map/ppermute | solution.py:310
  54.4 29.3 %collective-permute-start.22 = (bf16[256,768]{1,0:T(8,128)(2,1)S(1)}, bf16[256,768]{1,0:T(8,128)(2,1)S(1)}, u32[]{:S(2)}, u32[]{:S(2)}) collective-permute-start(bf16[256,768]{1,0:T(8,128)(2,1)S(1)} %shard_map.52.refs_6_), channel_id=1, source_target_pairs={{0,16},{4,20},{8,24},{12,28},{16,0},{20,4},{24,8},{28,12},{1,17},{... | collective-permute-start | bytes 1179656 | tf_op jit(solution)/shard_map/ppermute | solution.py:310
  59.0 24.9 %collective-permute-start.21 = (bf16[256,768]{1,0:T(8,128)(2,1)S(1)}, bf16[256,768]{1,0:T(8,128)(2,1)S(1)}, u32[]{:S(2)}, u32[]{:S(2)}) collective-permute-start(bf16[256,768]{1,0:T(8,128)(2,1)S(1)} %shard_map.52.refs_6_), channel_id=1, source_target_pairs={{0,8},{4,12},{8,0},{12,4},{16,24},{20,28},{24,16},{28,20},{1,9},{5... | collective-permute-start | bytes 1179656 | tf_op jit(solution)/shard_map/ppermute | solution.py:310
  72.5 23.3 %collective-permute-start.14 = (bf16[128,768]{1,0:T(8,128)(2,1)S(1)}, bf16[128,768]{1,0:T(8,128)(2,1)S(1)}, u32[]{:S(2)}, u32[]{:S(2)}) collective-permute-start(bf16[128,768]{1,0:T(8,128)(2,1)S(1)} %get-tuple-element.41), channel_id=1, source_target_pairs={{0,3},{1,2},{2,1},{3,0},{4,7},{5,6},{6,5},{7,4},{8,11},{9,10},{10,... | collective-permute-start | bytes 589832 | tf_op jit(solution)/shard_map/ppermute | solution.py:307
  85.0 6.2 %collective-permute-start.24 = (bf16[128,384]{1,0:T(8,128)(2,1)S(1)}, bf16[128,384]{1,0:T(8,128)(2,1)S(1)}, u32[]{:S(2)}, u32[]{:S(2)}) collective-permute-start(bf16[128,384]{1,0:T(8,128)(2,1)S(1)} %shard_map.55), channel_id=1, source_target_pairs={{0,4},{4,0},{8,12},{12,8},{16,20},{20,16},{24,28},{28,24},{1,5},{5... | collective-permute-start | bytes 294920 | tf_op jit(solution)/shard_map/ppermute | solution.py:310
  85.1 15.0 %collective-permute-start.15 = (bf16[128,768]{1,0:T(8,128)(2,1)S(1)}, bf16[128,768]{1,0:T(8,128)(2,1)S(1)}, u32[]{:S(2)}, u32[]{:S(2)}) collective-permute-start(bf16[128,768]{1,0:T(8,128)(2,1)S(1)} %get-tuple-element.42), channel_id=1, source_target_pairs={{0,2},{1,3},{2,0},{3,1},{4,6},{5,7},{6,4},{7,5},{8,10},{9,11},{10,... | collective-permute-start | bytes 589832 | tf_op jit(solution)/shard_map/ppermute | solution.py:307
  90.1 10.2 %collective-permute-start.16 = (bf16[128,768]{1,0:T(8,128)(2,1)S(1)}, bf16[128,768]{1,0:T(8,128)(2,1)S(1)}, u32[]{:S(2)}, u32[]{:S(2)}) collective-permute-start(bf16[128,768]{1,0:T(8,128)(2,1)S(1)} %get-tuple-element.43), channel_id=1, source_target_pairs={{0,1},{1,0},{2,3},{3,2},{4,5},{5,4},{6,7},{7,6},{8,9},{9,8},{10,11... | collective-permute-start | bytes 589832 | tf_op jit(solution)/shard_map/ppermute | solution.py:307
  92.3 13.5 %collective-permute-start.25 = (bf16[128,768]{1,0:T(8,128)(2,1)S(1)}, bf16[128,768]{1,0:T(8,128)(2,1)S(1)}, u32[]{:S(2)}, u32[]{:S(2)}) collective-permute-start(bf16[128,768]{1,0:T(8,128)(2,1)S(1)} %get-tuple-element.54), channel_id=1, source_target_pairs={{0,3},{1,2},{2,1},{3,0},{4,7},{5,6},{6,5},{7,4},{8,11},{9,10},{10,... | collective-permute-start | bytes 589832 | tf_op jit(solution)/shard_map/ppermute | solution.py:307
  93.9 22.9 %collective-permute-start.26 = (bf16[128,768]{1,0:T(8,128)(2,1)S(1)}, bf16[128,768]{1,0:T(8,128)(2,1)S(1)}, u32[]{:S(2)}, u32[]{:S(2)}) collective-permute-start(bf16[128,768]{1,0:T(8,128)(2,1)S(1)} %get-tuple-element.55), channel_id=1, source_target_pairs={{0,2},{1,3},{2,0},{3,1},{4,6},{5,7},{6,4},{7,5},{8,10},{9,11},{10,... | collective-permute-start | bytes 589832 | tf_op jit(solution)/shard_map/ppermute | solution.py:307
  95.8 20.9 %collective-permute-start.27 = (bf16[128,768]{1,0:T(8,128)(2,1)S(1)}, bf16[128,768]{1,0:T(8,128)(2,1)S(1)}, u32[]{:S(2)}, u32[]{:S(2)}) collective-permute-start(bf16[128,768]{1,0:T(8,128)(2,1)S(1)} %get-tuple-element.56), channel_id=1, source_target_pairs={{0,1},{1,0},{2,3},{3,2},{4,5},{5,4},{6,7},{7,6},{8,9},{9,8},{10,11... | collective-permute-start | bytes 589832 | tf_op jit(solution)/shard_map/ppermute | solution.py:307
  (13 other events, 147.2 us)
